TPU v7x, 512 devices: a whole 4x8x8 slice. The times are simulated.
512 devices in a mesh: grp: 16 (over y, core), blk: 32 (over z, x).
Axes of the slice: x: 4, y: 8, z: 8, core: 2. Of those that a mesh axis runs over, the one named last changes fastest.
Arguments:
- grads: bfloat16 [512, 4096, 128], P(('grp', 'blk')), may hold values from -6 to 6
- picks: int32 [512, 4096], P(('grp', 'blk')), may hold values from 0 to 511, as said below
- slot_map: int32 [512, 512], P(('grp', 'blk')), may hold values from 0 to 511, each once within a row
- momentum: float32 [262144, 128], P(('grp', 'blk')), may hold values from -6 to 6
- params: float32 [262144, 128], P(('grp', 'blk')), may hold values from -6 to 6
Outputs:
- new_momentum: float32 [262144, 128], P(('grp', 'blk'))
- new_params: float32 [262144, 128], P(('grp', 'blk'))
Inputs may be any that keep to these rules, and one draw needn't show every extreme that they name: `picks`: for each replica and owner, the 8 entries in order: the j-th lies in [j * 64, (j + 1) * 64). `slot_map`: each row is a permutation of the 512 slots.
All inputs are finite; a program needn't handle non-finite values.
Results may differ from a plain program's by a relative error of at most 0.0003.
Values may be sent and summed in bfloat16 or wider, within the bound.
No kernel may reach another device: no remote copies, remote signals or barrier semaphores. Data moves between devices by JAX's collectives and lax.ppermute only.
A program may use at most 64 MiB of HBM per device.

v0:
```python
import jax
import jax.numpy as jnp
from jax import lax
from jax.sharding import PartitionSpec as P


def cut_along(value, dim, size):
    lengths = value.shape
    blocks = value.reshape(*lengths[:dim], size, lengths[dim] // size, *lengths[dim + 1 :])
    return jnp.moveaxis(blocks, dim, 0)


def in_order(blocks, dim):
    lengths = list(blocks.shape[1:])
    lengths[dim] *= blocks.shape[0]
    return jnp.moveaxis(blocks, 0, dim).reshape(lengths)


def one_exchange(value, axis, axes, splits, concats):
    sizes = [lax.axis_size(a) for a in axes]
    blocks = cut_along(value, splits[0], sizes[0])
    blocks = jnp.moveaxis(cut_along(blocks, splits[1] + 1, sizes[1]), 0, 1)
    inside = blocks.shape[2:]
    blocks = blocks.reshape(-1, *inside)
    blocks = lax.all_to_all(blocks, axis, split_axis=0, concat_axis=0, tiled=True)
    blocks = in_order(blocks.reshape(*sizes, *inside), concats[0] + 1)
    return in_order(blocks, concats[1])


def densify(values, chosen, owned):
    numbers = lax.broadcasted_iota(jnp.int32, (1, owned, 1), 1)
    onehot = (chosen[:, None, :] == numbers).astype(jnp.bfloat16)
    return jnp.einsum("nrm,nmc->nrc", onehot, values, preferred_element_type=jnp.float32)


def attach_numbers(values, chosen):
    block = values.shape[-1]
    count = chosen.shape[-1]
    upper = (chosen // 16).astype(jnp.bfloat16)
    lower = (chosen % 16).astype(jnp.bfloat16)
    filler = jnp.zeros(chosen.shape[:-1] + (block - 2 * count,), jnp.bfloat16)
    number_row = jnp.concatenate([upper, lower, filler], axis=-1)
    return jnp.concatenate([values, number_row[..., None, :]], axis=-2)


def split_numbers(packed):
    count = packed.shape[-2] - 1
    values = packed[..., :count, :]
    number_row = packed[..., count, :]
    upper = number_row[..., :count].astype(jnp.float32)
    lower = number_row[..., count : 2 * count].astype(jnp.float32)
    chosen = (upper * 16.0 + lower).astype(jnp.int32)
    return (values, chosen)


def shards(grads, picks, slot_map, momentum, params):
    groups = lax.axis_size("grp")
    columns = lax.axis_size("blk")
    block = grads.shape[-1]
    owned = slot_map.shape[1]
    values = grads.reshape(groups, columns, -1, block)
    chosen = picks.reshape(groups, columns, -1)
    packed = attach_numbers(values, chosen)
    arrived = one_exchange(packed, ("grp", "blk"), ("grp", "blk"), (0, 1), (0, 1))
    arrived_values, arrived_chosen = split_numbers(arrived)
    merged = densify(arrived_values.reshape(1, -1, block), arrived_chosen.reshape(1, -1), owned)[0]
    slots = lax.broadcasted_iota(jnp.int32, (owned, owned), 0)
    placing = (slot_map[0][None, :] == slots).astype(jnp.float32)
    gradient = jnp.dot(
        placing, merged, precision=lax.Precision.HIGHEST, preferred_element_type=jnp.float32
    )
    new_momentum = 0.9 * momentum + gradient
    new_params = params - 0.05 * (gradient + 0.9 * new_momentum)
    return (new_momentum, new_params)


def solution(mesh):
    placed = (
        P(("grp", "blk"), None, None),
        P(("grp", "blk"), None),
        P(("grp", "blk"), None),
        P(("grp", "blk"), None),
        P(("grp", "blk"), None),
    )
    return jax.shard_map(
        shards,
        mesh=mesh,
        in_specs=placed,
        out_specs=(P(("grp", "blk"), None), P(("grp", "blk"), None)),
        check_vma=False,
    )
```

profile of v0, /device:TPU:1, one launch (start us, length us, event | category | flops | bytes accessed | tf_op | source)
XLA Modules:
  0.0 85.9 jit_solution(12041241249800076616)
XLA Ops:
  0.6 0.5 broadcast.86
  1.1 1.4 %reduce.3 = s32[4096]{0:T(1024)S(1)} reduce(s32[1,4096]{1,0:T(1,128)} %param.6, s32[]{:T(128)} %broadcast.86), dimensions={0}, to_apply=%param.6.reduce_sub_computation.3 | reduce | bytes 32772 | tf_op args[1]
  2.5 0.2 reshape.118
  2.7 0.1 copy.16
  2.8 0.2 copy.20
  3.0 0.2 copy.21
  3.2 0.1 pad.3.clone
  3.3 2.2 %maximum_maximum_fusion = bf16[512,1,1,9,128]{4,3,2,1,0:T(8,128)(2,1)S(1)} fusion(bf16[512,1,1,1,8]{4,3,2,1,0:T(2,128)(2,1)S(1)} %copy.21, bf16[512,1,1,1,8]{4,3,2,1,0:T(2,128)(2,1)S(1)} %copy.20, bf16[512,1,1,8,128]{4,3,2,1,0:T(8,128)(2,1)} %bitcast.19, bf16[9,128]{1,0:T(8,128)(2,1)S(1)} %pad.3.clone), kind=kLoop, calls=%fused_computation.3 | loop fusion | flops 4718592 | bytes 2246912 | tf_op jit(solution)/shard_map/concatenate | solution.py:43
  5.5 76.2 %all_to_all.5 = bf16[512,1,1,9,128]{4,3,2,1,0:T(8,128)(2,1)S(1)} all-to-all(bf16[512,1,1,9,128]{4,3,2,1,0:T(8,128)(2,1)S(1)} %maximum_maximum_fusion), channel_id=1, replica_groups=mesh['grp'=16,'blk'=32] {'grp','blk'}, dimensions={0} | all-to-all | bytes 2359296 | tf_op jit(solution)/shard_map/all_to_all | solution.py:25
  81.7 0.3 copy.22
  82.0 0.1 slice.19
  82.1 0.7 copy.23
  82.8 0.1 add_convert_fusion
  82.9 0.1 eq.34
  83.1 0.0 copy-start
  83.1 0.0 copy-start.1
  83.1 0.0 copy-start.2
  83.1 1.4 %fusion = f32[512,128]{1,0:T(8,128)S(1)} fusion(bf16[4096,128]{1,0:T(8,128)(2,1)S(1)} %bitcast.18, s32[4096]{0:T(1024)S(1)} %eq.34), kind=kOutput, calls=%fused_computation.1 | convolution fusion | flops 538968064 | bytes 1327104 | tf_op jit(solution)/shard_map/nrm,nmc->nrc/dot_general | solution.py:33
  84.5 0.0 copy-done
  84.5 0.0 copy-done.1
  84.5 0.0 copy-done.2
  84.5 1.4 %multiply_subtract_fusion = (f32[512,128]{1,0:T(8,128)}, f32[512,128]{1,0:T(8,128)}) fusion(f32[512,128]{1,0:T(8,128)S(1)} %copy-done, f32[512,128]{1,0:T(8,128)S(1)} %copy-done.1, f32[512,128]{1,0:T(8,128)S(1)} %fusion, s32[512]{0:T(512)S(1)} %bitcast.20), kind=kOutput, calls=%fused_computation.7 | convolution fusion | flops 403308544 | bytes 1312768 | tf_op jit(solution)/shard_map/dot_general | solution.py:69
  (3 shorter events, 0.0 us)
Async XLA Ops:
  83.1 1.4 %copy-start = (f32[512,128]{1,0:T(8,128)S(1)}, f32[512,128]{1,0:T(8,128)}, u32[]{:S(2)}) copy-start(f32[512,128]{1,0:T(8,128)} %param.9) | copy-start | bytes 786436
  83.1 1.4 %copy-start.1 = (f32[512,128]{1,0:T(8,128)S(1)}, f32[512,128]{1,0:T(8,128)}, u32[]{:S(2)}) copy-start(f32[512,128]{1,0:T(8,128)} %param.8) | copy-start | bytes 786436
  83.1 1.4 %copy-start.2 = (s32[1,512]{1,0:T(1,128)S(1)}, s32[1,512]{1,0:T(1,128)}, u32[]{:S(2)}) copy-start(s32[1,512]{1,0:T(1,128)} %param.7) | copy-start | bytes 6148
where the time goes:
time: 86.2 us; the launch traced here: 85.9 us
  blocking collectives  76.2 us (88%)
  other arithmetic  3.75 us (4%)
  matrix products  2.8 us (3%)
  local copies, waits for them, and re-layouts  2.42 us (3%)
    all_to_all x1, blocking collectives, one_exchange(): lax.all_to_all(blocks, axis, split_axis=0, concat_axis=0, tiled=True)  76.2 us
    concatenate x1, other arithmetic, attach_numbers(): return jnp.concatenate([values, number_row[..., None, :]], axis=-2)  2.21 us

commit v1 on v0

v1 whole, which is shorter than its diff:
```python
import functools

import jax
import jax.numpy as jnp
from jax import lax
from jax.experimental import pallas as pl
from jax.experimental.pallas import tpu as pltpu
from jax.sharding import PartitionSpec as P

PAIR = 2
VMEM_LIMIT = 16 * 1024 * 1024


def pack(owners, tiles, window, grads_ref, picks_ref, out_ref, sem):
    copy = pltpu.make_async_copy(grads_ref, out_ref.at[:, 0:tiles], sem)
    copy.start()
    rows = picks_ref.shape[0]
    share = owners // rows
    offsets = lax.rem(picks_ref[...], window).astype(jnp.float32).astype(jnp.bfloat16)
    for r in range(rows):
        row = jnp.broadcast_to(offsets[r : r + 1][None], (share, PAIR, offsets.shape[1]))
        out_ref[r * share : (r + 1) * share, tiles] = row
    copy.wait()


def regroup(tiles, in_ref, out_ref, sems):
    copies = [pltpu.make_async_copy(in_ref.at[:, k], out_ref.at[k], sems.at[k]) for k in range(tiles + 1)]
    for copy in copies:
        copy.start()
    for copy in copies:
        copy.wait()


def update(
    pick, window, share, got_ref, slots_ref, mom_ref, par_ref, new_mom_ref, new_par_ref, numbers_ref
):
    tiles = pick // PAIR
    owned, block = mom_ref.shape
    count = got_ref.shape[1]
    numbers_ref[...] = got_ref[tiles].astype(jnp.float32).T
    first = lax.rem(lax.axis_index("blk"), share) * pick
    mine = numbers_ref[pl.ds(pl.multiple_of(first, pick), pick), :]
    lane = lax.broadcasted_iota(jnp.int32, (1, count), 1)
    odd = lax.rem(lane, PAIR) == 1
    place = lax.broadcasted_iota(jnp.int32, (PAIR * window, count), 0).astype(jnp.float32)
    parts = []
    for k in range(tiles):
        key = jnp.where(odd, mine[PAIR * k + 1 : PAIR * k + 2] + float(window), mine[PAIR * k : PAIR * k + 1])
        onehot = jnp.where(place == key, 1.0, 0.0).astype(jnp.bfloat16)
        parts.append(jnp.dot(onehot, got_ref[k], preferred_element_type=jnp.float32))
    merged = jnp.concatenate(parts, axis=0)
    high = merged.astype(jnp.bfloat16)
    rest = merged - high.astype(jnp.float32)
    middle = rest.astype(jnp.bfloat16)
    low = (rest - middle.astype(jnp.float32)).astype(jnp.bfloat16)
    slots = lax.broadcasted_iota(jnp.int32, (owned, owned), 0)
    placing = jnp.where(slots == slots_ref[...], 1.0, 0.0).astype(jnp.bfloat16)
    sums = jnp.dot(
        placing, jnp.concatenate([high, middle, low], axis=1), preferred_element_type=jnp.float32
    )
    gradient = sums[:, :block] + (sums[:, block : 2 * block] + sums[:, 2 * block :])
    new_momentum = 0.9 * mom_ref[...] + gradient
    new_mom_ref[...] = new_momentum
    new_par_ref[...] = par_ref[...] - 0.05 * (gradient + 0.9 * new_momentum)


def shards(grads, picks, slot_map, momentum, params):
    devices = lax.axis_size("grp") * lax.axis_size("blk")
    items, block = grads.shape[1:]
    owned = slot_map.shape[1]
    pick = items // devices
    tiles = pick // PAIR
    window = owned // pick
    rows = items // block
    vmem = pl.BlockSpec(memory_space=pltpu.VMEM)
    anywhere = pl.BlockSpec(memory_space=pl.ANY)
    distant = pl.BlockSpec(memory_space=pltpu.HBM)
    params_of = pltpu.CompilerParams(vmem_limit_bytes=VMEM_LIMIT)
    packed = pl.pallas_call(
        functools.partial(pack, devices, tiles, window),
        out_shape=jax.ShapeDtypeStruct((devices, tiles + 1, PAIR, block), grads.dtype),
        in_specs=[distant, vmem],
        out_specs=vmem,
        scratch_shapes=[pltpu.SemaphoreType.DMA],
        compiler_params=params_of,
        name="pack",
    )(grads.reshape(devices, tiles, PAIR, block), picks.reshape(rows, block))
    arrived = lax.all_to_all(packed, ("grp", "blk"), split_axis=0, concat_axis=0, tiled=True)
    grouped = pl.pallas_call(
        functools.partial(regroup, tiles),
        out_shape=jax.ShapeDtypeStruct((tiles + 1, devices, PAIR, block), grads.dtype),
        in_specs=[anywhere],
        out_specs=vmem,
        scratch_shapes=[pltpu.SemaphoreType.DMA((tiles + 1,))],
        compiler_params=params_of,
        name="regroup",
    )(arrived)
    return pl.pallas_call(
        functools.partial(update, pick, window, devices // rows),
        out_shape=(
            jax.ShapeDtypeStruct(momentum.shape, jnp.float32),
            jax.ShapeDtypeStruct(params.shape, jnp.float32),
        ),
        in_specs=[vmem] * 4,
        out_specs=(vmem, vmem),
        scratch_shapes=[pltpu.VMEM((block, PAIR * devices), jnp.float32)],
        compiler_params=params_of,
        name="update",
    )(grouped.reshape(tiles + 1, PAIR * devices, block), slot_map, momentum, params)


def solution(mesh):
    placed = (
        P(("grp", "blk"), None, None),
        P(("grp", "blk"), None),
        P(("grp", "blk"), None),
        P(("grp", "blk"), None),
        P(("grp", "blk"), None),
    )
    return jax.shard_map(
        shards,
        mesh=mesh,
        in_specs=placed,
        out_specs=(P(("grp", "blk"), None), P(("grp", "blk"), None)),
        check_vma=False,
    )
```

time: 86.2 us -> 66.2 us (0.77)
  blocking collectives: 76.2 us -> 60.4 us
  other arithmetic: 3.75 us -> 0 us
  Pallas kernels: 0 us -> 2.9 us
  matrix products: 2.8 us -> 0 us
    all_to_all x1, blocking collectives: 76.2 us -> 60.4 us  [shards(): lax.all_to_all(packed, ('grp', 'blk'), split_axis=0, concat_axis=0, tiled...]
    pallas_call x0 -> x3, Pallas kernels: none -> 2.9 us  [the longest x1 1.61 us: shards(): pl.pallas_call(functools.partial(update, pick, window, devices // rows),...]
    dot_general x2 -> x0, matrix products: 2.8 us -> none  [the longest x1 1.41 us: shards(): jnp.dot(placing, merged, precision=lax.Precision.HIGHEST, preferred_eleme...]
    concatenate x1 -> x0, other arithmetic: 2.21 us -> none  [attach_numbers(): return jnp.concatenate([values, number_row[..., None, :]], axis=-2)]
    unnamed x7 -> x10, local copies, waits for them, and re-layouts: 0.53 us -> 2 us
    unnamed x1 -> x0, other arithmetic: 1.4 us -> none
where the time goes in v1:
time: 66.2 us; the launch traced here: 65.9 us
  blocking collectives  60.4 us (91%)
  Pallas kernels  2.9 us (4%)
  local copies, waits for them, and re-layouts  2 us (3%)
  between operations  0.67 us (1%)
    all_to_all x1, blocking collectives, shards(): lax.all_to_all(packed, ('grp', 'blk'), split_axis=0, concat_axis=0, tiled...  60.4 us
    unnamed x10, local copies, waits for them, and re-layouts  2 us
    pallas_call x1, Pallas kernels, shards(): pl.pallas_call(functools.partial(update, pick, window, devices // rows),...  1.61 us

profile of v1, /device:TPU:1, one launch (start us, length us, event | category | flops | bytes accessed | tf_op | source)
XLA Modules:
  0.0 65.9 jit_solution(15177166242451912660)
XLA Ops:
  0.6 0.0 copy-start
  0.6 1.2 %copy-done = bf16[1,4096,128]{2,1,0:T(8,128)(2,1)S(1)} copy-done((bf16[1,4096,128]{2,1,0:T(8,128)(2,1)S(1)}, bf16[1,4096,128]{2,1,0:T(8,128)(2,1)}, u32[]{:S(2)}) %copy-start) | copy-done | bytes 1048600
  1.9 0.0 copy-start.3
  1.9 0.7 %copy-done.3 = s32[1,4096]{1,0:T(1,128)S(1)} copy-done((s32[1,4096]{1,0:T(1,128)S(1)}, s32[1,4096]{1,0:T(1,128)}, u32[]{:S(2)}) %copy-start.3) | copy-done | bytes 16408
  2.6 0.3 pack.1
  2.9 60.4 %all_to_all.5.in_ref = bf16[512,5,2,128]{3,2,1,0:T(2,128)(2,1)S(1)} all-to-all(bf16[512,5,2,128]{3,2,1,0:T(2,128)(2,1)S(1)} %pack.1), channel_id=1, replica_groups=mesh['grp'=16,'blk'=32] {'grp','blk'}, dimensions={0} | all-to-all | bytes 2621440 | tf_op jit(solution)/shard_map/all_to_all | solution.py:88
  63.3 0.0 copy-start.1
  63.3 0.0 copy-start.2
  63.3 0.0 copy-start.4
  63.3 1.0 %regroup.1 = bf16[5,512,2,128]{3,2,1,0:T(2,128)(2,1)S(1)} custom-call(bf16[512,5,2,128]{3,2,1,0:T(2,128)(2,1)S(1)} %all_to_all.5.in_ref), custom_call_target="tpu_custom_call" | custom-call | tf_op jit(solution)/shard_map/regroup/pallas_call | solution.py:89
  64.2 0.0 copy-done.1
  64.2 0.1 copy-done.2
  64.3 0.0 copy-done.4
  64.3 1.6 %update.1 = (f32[512,128]{1,0:T(8,128)}, f32[512,128]{1,0:T(8,128)}) custom-call(bf16[5,1024,128]{2,1,0:T(8,128)(2,1)S(1)} %bitcast.3, s32[1,512]{1,0:T(1,128)S(1)} %copy-done.4, f32[512,128]{1,0:T(8,128)S(1)} %copy-done.1, f32[512,128]{1,0:T(8,128)S(1)} %copy-done.2), custom_call_target="tpu_custom_call" | custom-call | tf_op jit(solution)/shard_map/update/pallas_call | solution.py:98
Async XLA Ops:
  0.6 1.2 %copy-start = (bf16[1,4096,128]{2,1,0:T(8,128)(2,1)S(1)}, bf16[1,4096,128]{2,1,0:T(8,128)(2,1)}, u32[]{:S(2)}) copy-start(bf16[1,4096,128]{2,1,0:T(8,128)(2,1)} %param.5) | copy-start | bytes 3145732
  1.9 0.7 %copy-start.3 = (s32[1,4096]{1,0:T(1,128)S(1)}, s32[1,4096]{1,0:T(1,128)}, u32[]{:S(2)}) copy-start(s32[1,4096]{1,0:T(1,128)} %param.6) | copy-start | bytes 49156
  63.3 1.0 %copy-start.1 = (f32[512,128]{1,0:T(8,128)S(1)}, f32[512,128]{1,0:T(8,128)}, u32[]{:S(2)}) copy-start(f32[512,128]{1,0:T(8,128)} %mom_ref.1) | copy-start | bytes 786436
  63.3 1.0 %copy-start.2 = (f32[512,128]{1,0:T(8,128)S(1)}, f32[512,128]{1,0:T(8,128)}, u32[]{:S(2)}) copy-start(f32[512,128]{1,0:T(8,128)} %par_ref.1) | copy-start | bytes 786436
  63.3 1.0 %copy-start.4 = (s32[1,512]{1,0:T(1,128)S(1)}, s32[1,512]{1,0:T(1,128)}, u32[]{:S(2)}) copy-start(s32[1,512]{1,0:T(1,128)} %slots_ref.1) | copy-start | bytes 6148

commit v2 on v1

v2 whole, which is shorter than its diff:
```python
import functools

import jax
import jax.numpy as jnp
from jax import lax
from jax.experimental import pallas as pl
from jax.experimental.pallas import tpu as pltpu
from jax.sharding import PartitionSpec as P

PAIR = 2
VMEM_LIMIT = 16 * 1024 * 1024


def pack(owners, tiles, window, grads_ref, picks_ref, out_ref, numbers_ref, sems):
    read = pltpu.make_async_copy(picks_ref, numbers_ref, sems.at[0])
    copy = pltpu.make_async_copy(grads_ref, out_ref.at[:, 0:tiles], sems.at[1])
    read.start()
    copy.start()
    read.wait()
    rows = numbers_ref.shape[0]
    share = owners // rows
    offsets = lax.rem(numbers_ref[...], window).astype(jnp.float32).astype(jnp.bfloat16)
    for r in range(rows):
        row = jnp.broadcast_to(offsets[r : r + 1][None], (share, PAIR, offsets.shape[1]))
        out_ref[r * share : (r + 1) * share, tiles] = row
    copy.wait()


def regroup(tiles, got_ref, slots_ref, out_ref, placing_ref, sems):
    copies = [pltpu.make_async_copy(got_ref.at[:, k], out_ref.at[k], sems.at[k]) for k in range(tiles + 1)]
    for copy in copies:
        copy.start()
    numbered = lax.broadcasted_iota(jnp.int32, placing_ref.shape, 0)
    placing_ref[...] = jnp.where(numbered == slots_ref[...], 1.0, 0.0).astype(jnp.bfloat16)
    for copy in copies:
        copy.wait()


def update(pick, window, share, got, placing, mom, par, new_mom, new_par, numbers):
    tiles = pick // PAIR
    owned, block = mom.shape
    count = got.shape[1]
    first = lax.rem(lax.axis_index("blk"), share) * pick
    numbers[...] = got[tiles].astype(jnp.float32).T
    mine = numbers[pl.ds(pl.multiple_of(first, pick), pick), :]
    lane = lax.broadcasted_iota(jnp.int32, (1, count), 1)
    odd = lax.rem(lane, PAIR) == 1
    place = lax.broadcasted_iota(jnp.int32, (PAIR * window, count), 0).astype(jnp.float32)
    parts = []
    for k in range(tiles):
        key = jnp.where(odd, mine[PAIR * k + 1 : PAIR * k + 2] + float(window), mine[PAIR * k : PAIR * k + 1])
        onehot = jnp.where(place == key, 1.0, 0.0).astype(jnp.bfloat16)
        parts.append(jnp.dot(onehot, got[k], preferred_element_type=jnp.float32))
    merged = jnp.concatenate(parts, axis=0)
    high = merged.astype(jnp.bfloat16)
    rest = merged - high.astype(jnp.float32)
    middle = rest.astype(jnp.bfloat16)
    low = (rest - middle.astype(jnp.float32)).astype(jnp.bfloat16)
    pieces = jnp.concatenate([high, middle, low], axis=1)
    sums = jnp.dot(placing[...], pieces, preferred_element_type=jnp.float32)
    gradient = sums[:, :block] + (sums[:, block : 2 * block] + sums[:, 2 * block :])
    new_momentum = 0.9 * mom[...] + gradient
    new_mom[...] = new_momentum
    new_par[...] = par[...] - 0.05 * (gradient + 0.9 * new_momentum)


def shards(grads, picks, slot_map, momentum, params):
    devices = lax.axis_size("grp") * lax.axis_size("blk")
    items, block = grads.shape[1:]
    owned = slot_map.shape[1]
    pick = items // devices
    tiles = pick // PAIR
    window = owned // pick
    rows = items // block
    vmem = pl.BlockSpec(memory_space=pltpu.VMEM)
    distant = pl.BlockSpec(memory_space=pltpu.HBM)
    in_hbm = functools.partial(pltpu.with_memory_space_constraint, memory_space=pltpu.HBM)
    limits = pltpu.CompilerParams(vmem_limit_bytes=VMEM_LIMIT)
    packed = pl.pallas_call(
        functools.partial(pack, devices, tiles, window),
        out_shape=jax.ShapeDtypeStruct((devices, tiles + 1, PAIR, block), grads.dtype),
        in_specs=[distant, distant],
        out_specs=vmem,
        scratch_shapes=[pltpu.VMEM((rows, block), jnp.int32), pltpu.SemaphoreType.DMA((2,))],
        compiler_params=limits,
        name="pack",
    )(in_hbm(grads.reshape(devices, tiles, PAIR, block)), in_hbm(picks.reshape(rows, block)))
    arrived = lax.all_to_all(packed, ("grp", "blk"), split_axis=0, concat_axis=0, tiled=True)
    grouped, placing = pl.pallas_call(
        functools.partial(regroup, tiles),
        out_shape=(
            jax.ShapeDtypeStruct((tiles + 1, devices, PAIR, block), grads.dtype),
            jax.ShapeDtypeStruct((owned, owned), jnp.bfloat16),
        ),
        in_specs=[vmem, vmem],
        out_specs=(vmem, vmem),
        scratch_shapes=[pltpu.SemaphoreType.DMA((tiles + 1,))],
        compiler_params=limits,
        name="regroup",
    )(arrived, slot_map)
    return pl.pallas_call(
        functools.partial(update, pick, window, devices // rows),
        out_shape=(
            jax.ShapeDtypeStruct(momentum.shape, jnp.float32),
            jax.ShapeDtypeStruct(params.shape, jnp.float32),
        ),
        in_specs=[vmem] * 4,
        out_specs=(vmem, vmem),
        scratch_shapes=[
            pltpu.VMEM((block, PAIR * devices), jnp.float32),
        ],
        compiler_params=limits,
        name="update",
    )(grouped.reshape(tiles + 1, PAIR * devices, block), placing, momentum, params)


def solution(mesh):
    placed = (
        P(("grp", "blk"), None, None),
        P(("grp", "blk"), None),
        P(("grp", "blk"), None),
        P(("grp", "blk"), None),
        P(("grp", "blk"), None),
    )
    return jax.shard_map(
        shards,
        mesh=mesh,
        in_specs=placed,
        out_specs=(P(("grp", "blk"), None), P(("grp", "blk"), None)),
        check_vma=False,
    )
```

time: 66.2 us -> 65.2 us (0.985)
  local copies, waits for them, and re-layouts: 2 us -> 0.01 us
  Pallas kernels: 2.9 us -> 3.93 us
    unnamed x10 -> x6, local copies, waits for them, and re-layouts: 2 us -> 0.01 us
    pallas_call x1, Pallas kernels: 0.33 us -> 1.26 us  [shards(): pl.pallas_call(functools.partial(pack, devices, tiles, window), out_shape...]
where the time goes in v2:
time: 65.2 us; the launch traced here: 65 us
  blocking collectives  60.4 us (93%)
  Pallas kernels  3.93 us (6%)
  between operations  0.67 us (1%)
    all_to_all x1, blocking collectives, shards(): lax.all_to_all(packed, ('grp', 'blk'), split_axis=0, concat_axis=0, tiled...  60.4 us
    pallas_call x1, Pallas kernels, shards(): pl.pallas_call(functools.partial(update, pick, window, devices // rows),...  1.62 us

profile of v2, /device:TPU:1, one launch (start us, length us, event | category | flops | bytes accessed | tf_op | source)
XLA Modules:
  0.0 65.0 jit_solution(4303605779966302269)
XLA Ops:
  0.6 1.3 %pack.1 = bf16[512,5,2,128]{3,2,1,0:T(2,128)(2,1)S(1)} custom-call(bf16[512,4,2,128]{3,2,1,0:T(2,128)(2,1)} %bitcast.4, s32[32,128]{1,0:T(8,128)} %bitcast.5), custom_call_target="tpu_custom_call" | custom-call | tf_op jit(solution)/shard_map/pack/pallas_call | solution.py:79
  1.9 0.0 copy-start.2
  1.9 60.4 %all_to_all.5.got_ref = bf16[512,5,2,128]{3,2,1,0:T(2,128)(2,1)S(1)} all-to-all(bf16[512,5,2,128]{3,2,1,0:T(2,128)(2,1)S(1)} %pack.1), channel_id=1, replica_groups=mesh['grp'=16,'blk'=32] {'grp','blk'}, dimensions={0} | all-to-all | bytes 2621440 | tf_op jit(solution)/shard_map/all_to_all | solution.py:88
  62.3 0.0 copy-done.2
  62.3 0.0 copy-start
  62.3 0.0 copy-start.1
  62.3 1.1 %regroup.1 = (bf16[5,512,2,128]{3,2,1,0:T(2,128)(2,1)S(1)}, bf16[512,512]{1,0:T(8,128)(2,1)S(1)}) custom-call(bf16[512,5,2,128]{3,2,1,0:T(2,128)(2,1)S(1)} %all_to_all.5.got_ref, s32[1,512]{1,0:T(1,128)S(1)} %copy-done.2), custom_call_target="tpu_custom_call" | custom-call | tf_op jit(solution)/shard_map/regroup/pallas_call | solution.py:89
  63.3 0.0 copy-done
  63.3 0.0 copy-done.1
  63.3 1.6 %update.1 = (f32[512,128]{1,0:T(8,128)}, f32[512,128]{1,0:T(8,128)}) custom-call(bf16[5,1024,128]{2,1,0:T(8,128)(2,1)S(1)} %bitcast.3, bf16[512,512]{1,0:T(8,128)(2,1)S(1)} %get-tuple-element.5.placing, f32[512,128]{1,0:T(8,128)S(1)} %copy-done, f32[512,128]{1,0:T(8,128)S(1)} %copy-done.1), custom_call_target="tpu_custom_call" | custom-call | tf_op jit(solution)/shard_map/update/pallas_call | solution.py:101
Async XLA Ops:
  1.9 60.4 %copy-start.2 = (s32[1,512]{1,0:T(1,128)S(1)}, s32[1,512]{1,0:T(1,128)}, u32[]{:S(2)}) copy-start(s32[1,512]{1,0:T(1,128)} %slots_ref.1) | copy-start | bytes 6148
  62.3 1.1 %copy-start = (f32[512,128]{1,0:T(8,128)S(1)}, f32[512,128]{1,0:T(8,128)}, u32[]{:S(2)}) copy-start(f32[512,128]{1,0:T(8,128)} %mom.1) | copy-start | bytes 786436
  62.3 1.1 %copy-start.1 = (f32[512,128]{1,0:T(8,128)S(1)}, f32[512,128]{1,0:T(8,128)}, u32[]{:S(2)}) copy-start(f32[512,128]{1,0:T(8,128)} %par.1) | copy-start | bytes 786436

commit v3 on v2

v3 whole, which is shorter than its diff:
```python
import functools

import jax
import jax.numpy as jnp
from jax import lax
from jax.experimental import pallas as pl
from jax.experimental.pallas import tpu as pltpu
from jax.sharding import PartitionSpec as P

PAIR = 2
VMEM_LIMIT = 16 * 1024 * 1024


def pack(tiles, window, grads_ref, picks_ref, out_ref, numbers_ref, sems):
    read = pltpu.make_async_copy(picks_ref, numbers_ref, sems.at[PAIR])
    copies = [
        pltpu.make_async_copy(
            grads_ref.at[:, side], out_ref.at[:, :, side * tiles : (side + 1) * tiles], sems.at[side]
        )
        for side in range(PAIR)
    ]
    read.start()
    for copy in copies:
        copy.start()
    read.wait()
    groups, columns = out_ref.shape[:2]
    rows = numbers_ref.shape[0] // (PAIR * groups)
    share = columns // rows
    offsets = lax.rem(numbers_ref[...], window).astype(jnp.float32)
    for g in range(groups):
        for r in range(rows):
            at = [(g * PAIR + side) * rows + r for side in range(PAIR)]
            two = jnp.concatenate([offsets[a : a + 1] for a in at], axis=0).astype(jnp.bfloat16)
            out_ref[g, r * share : (r + 1) * share, PAIR * tiles] = jnp.broadcast_to(
                two[None], (share,) + two.shape
            )
    for copy in copies:
        copy.wait()


def side_of(mine):
    core = lax.rem(lax.axis_index("grp"), PAIR)
    return core if mine else 1 - core


def regroup_theirs(tiles, got_ref, out_ref, sems):
    start = side_of(False) * tiles
    at = [start + k for k in range(tiles)] + [PAIR * tiles]
    copies = [pltpu.make_async_copy(got_ref.at[:, t], out_ref.at[k], sems.at[k]) for k, t in enumerate(at)]
    for copy in copies:
        copy.start()
    for copy in copies:
        copy.wait()


def regroup_mine(tiles, got_ref, slots_ref, out_ref, placing_ref, sems):
    start = side_of(True) * tiles
    copies = [pltpu.make_async_copy(got_ref.at[:, start + k], out_ref.at[k], sems.at[k]) for k in range(tiles)]
    for copy in copies:
        copy.start()
    numbered = lax.broadcasted_iota(jnp.int32, placing_ref.shape, 0)
    placing_ref[...] = jnp.where(numbered == slots_ref[...], 1.0, 0.0).astype(jnp.bfloat16)
    for copy in copies:
        copy.wait()


def add_up(mine, pick, window, share, got, theirs, sums, numbers):
    tiles = pick // PAIR
    count = got.shape[1]
    side = side_of(mine)
    numbers[...] = theirs[tiles].astype(jnp.float32).T
    first = lax.rem(lax.axis_index("blk"), share) * pick
    both = numbers[pl.ds(pl.multiple_of(first, pick), pick), :]
    odd = lax.rem(lax.broadcasted_iota(jnp.int32, (1, count), 1), PAIR)
    beside = jnp.where(side == 0, pltpu.roll(both, 1, 1), pltpu.roll(both, count - 1, 1))
    chosen = jnp.where(odd == side, both, beside)
    place = lax.broadcasted_iota(jnp.int32, (PAIR * window, count), 0).astype(jnp.float32)
    for k in range(tiles):
        key = jnp.where(odd == 1, chosen[PAIR * k + 1 : PAIR * k + 2] + float(window), chosen[PAIR * k : PAIR * k + 1])
        onehot = jnp.where(place == key, 1.0, 0.0).astype(jnp.bfloat16)
        sums[PAIR * window * k : PAIR * window * (k + 1)] = jnp.dot(
            onehot, got[k], preferred_element_type=jnp.float32
        )


def update(here, there, placing, mom, par, new_mom, new_par):
    block = mom.shape[1]
    merged = here[...] + there[...]
    high = merged.astype(jnp.bfloat16)
    rest = merged - high.astype(jnp.float32)
    middle = rest.astype(jnp.bfloat16)
    low = (rest - middle.astype(jnp.float32)).astype(jnp.bfloat16)
    pieces = jnp.concatenate([high, middle, low], axis=1)
    sums = jnp.dot(placing[...], pieces, preferred_element_type=jnp.float32)
    gradient = sums[:, :block] + (sums[:, block : 2 * block] + sums[:, 2 * block :])
    new_momentum = 0.9 * mom[...] + gradient
    new_mom[...] = new_momentum
    new_par[...] = par[...] - 0.05 * (gradient + 0.9 * new_momentum)


def shards(grads, picks, slot_map, momentum, params):
    groups, columns = lax.axis_size("grp"), lax.axis_size("blk")
    items, block = grads.shape[1:]
    owned = slot_map.shape[1]
    pick = items // (groups * columns)
    tiles = pick // PAIR
    window = owned // pick
    share = block // pick
    pairs = groups // PAIR
    sources = pairs * columns
    vmem = pl.BlockSpec(memory_space=pltpu.VMEM)
    distant = pl.BlockSpec(memory_space=pltpu.HBM)
    in_hbm = functools.partial(pltpu.with_memory_space_constraint, memory_space=pltpu.HBM)
    limits = pltpu.CompilerParams(vmem_limit_bytes=VMEM_LIMIT)
    packed = pl.pallas_call(
        functools.partial(pack, tiles, window),
        out_shape=jax.ShapeDtypeStruct((pairs, columns, PAIR * tiles + 1, PAIR, block), grads.dtype),
        in_specs=[distant, distant],
        out_specs=vmem,
        scratch_shapes=[pltpu.VMEM((items // block, block), jnp.int32), pltpu.SemaphoreType.DMA((PAIR + 1,))],
        compiler_params=limits,
        name="pack",
    )(
        in_hbm(grads.reshape(pairs, PAIR, columns, tiles, PAIR, block)),
        in_hbm(picks.reshape(items // block, block)),
    )
    arrived = lax.all_to_all(
        packed.reshape(sources, PAIR * tiles + 1, PAIR, block),
        ("grp", "blk"),
        split_axis=0,
        concat_axis=0,
        tiled=True,
        axis_index_groups=[
            [(g * PAIR + side) * columns + b for g in range(pairs) for b in range(columns)]
            for side in range(PAIR)
        ],
    )

    def summed(mine, values, theirs):
        return pl.pallas_call(
            functools.partial(add_up, mine, pick, window, share),
            out_shape=jax.ShapeDtypeStruct(momentum.shape, jnp.float32),
            in_specs=[vmem, vmem],
            out_specs=vmem,
            scratch_shapes=[pltpu.VMEM((block, PAIR * sources), jnp.float32)],
            compiler_params=limits,
            cost_estimate=pl.CostEstimate(
                flops=2 * owned * PAIR * sources * block, bytes_accessed=items * block * 2, transcendentals=0
            ),
            name="sum_mine" if mine else "sum_theirs",
        )(values, theirs)

    theirs = pl.pallas_call(
        functools.partial(regroup_theirs, tiles),
        out_shape=jax.ShapeDtypeStruct((tiles + 1, sources, PAIR, block), grads.dtype),
        in_specs=[vmem],
        out_specs=vmem,
        scratch_shapes=[pltpu.SemaphoreType.DMA((tiles + 1,))],
        compiler_params=limits,
        name="regroup_theirs",
    )(arrived).reshape(tiles + 1, PAIR * sources, block)
    there = lax.ppermute(summed(False, theirs, theirs), "grp", [(g, g ^ 1) for g in range(groups)])
    ours, placing = pl.pallas_call(
        functools.partial(regroup_mine, tiles),
        out_shape=(
            jax.ShapeDtypeStruct((tiles, sources, PAIR, block), grads.dtype),
            jax.ShapeDtypeStruct((owned, owned), jnp.bfloat16),
        ),
        in_specs=[vmem, vmem],
        out_specs=(vmem, vmem),
        scratch_shapes=[pltpu.SemaphoreType.DMA((tiles,))],
        compiler_params=limits,
        cost_estimate=pl.CostEstimate(flops=owned * owned * block, bytes_accessed=items * block * 2, transcendentals=0),
        name="regroup_mine",
    )(arrived, slot_map)
    here = summed(True, ours.reshape(tiles, PAIR * sources, block), theirs)
    return pl.pallas_call(
        update,
        out_shape=(
            jax.ShapeDtypeStruct(momentum.shape, jnp.float32),
            jax.ShapeDtypeStruct(params.shape, jnp.float32),
        ),
        in_specs=[vmem] * 5,
        out_specs=(vmem, vmem),
        compiler_params=limits,
        name="update",
    )(here, there, placing, momentum, params)


def solution(mesh):
    placed = (
        P(("grp", "blk"), None, None),
        P(("grp", "blk"), None),
        P(("grp", "blk"), None),
        P(("grp", "blk"), None),
        P(("grp", "blk"), None),
    )
    return jax.shard_map(
        shards,
        mesh=mesh,
        in_specs=placed,
        out_specs=(P(("grp", "blk"), None), P(("grp", "blk"), None)),
        check_vma=False,
    )
```

time: 65.2 us -> 64.8 us (level)
  blocking collectives: 60.4 us -> 54.1 us
  starting transfers between devices: 0 us -> 5.16 us
    all_to_all x1, blocking collectives: 60.4 us -> 54.1 us  [shards(): lax.all_to_all(packed.reshape(sources, PAIR * tiles + 1, PAIR, block), ('...]
    ppermute x0 -> x1, starting transfers between devices: none -> 5.16 us  [shards(): lax.ppermute(summed(False, theirs, theirs), 'grp', [(g, g ^ 1) for g in r...]
    pallas_call x3 -> x6, Pallas kernels: 3.93 us -> 4.45 us  [the longest x1 1.25 us: shards(): pl.pallas_call(update, out_shape=(jax.ShapeDtypeStruct(momentum.shape, jn...]
  transfers between devices with their start and end apart: 0 -> 1, of which waited for: 0 -> 1; matrix products, arithmetic and copies ran while one was open for 0% -> 0% of each run, Pallas kernels for 0% -> 2%
where the time goes in v3:
time: 64.8 us; the launch traced here: 64.6 us
  blocking collectives  54.1 us (83%)
  starting transfers between devices  5.16 us (8%)
  Pallas kernels  4.45 us (7%)
  between operations  0.71 us (1%)
    all_to_all x1, blocking collectives, shards(): lax.all_to_all(packed.reshape(sources, PAIR * tiles + 1, PAIR, block), ('...  54.1 us
    ppermute x1, starting transfers between devices, shards(): lax.ppermute(summed(False, theirs, theirs), 'grp', [(g, g ^ 1) for g in r...  5.16 us
  transfers between devices with their start and end apart: 1, of which 1 were waited for; matrix products, arithmetic and copies ran while one was open for 0% of the time, Pallas kernels for 2%

profile of v3, /device:TPU:1, one launch (start us, length us, event | category | flops | bytes accessed | tf_op | source)
XLA Modules:
  0.0 64.6 jit_solution(10690310685648638705)
XLA Ops:
  0.6 1.2 %pack.1 = bf16[8,32,9,2,128]{4,3,2,1,0:T(2,128)(2,1)S(1)} custom-call(bf16[8,2,32,4,2,128]{5,4,3,2,1,0:T(2,128)(2,1)} %bitcast.10, s32[32,128]{1,0:T(8,128)} %bitcast.11), custom_call_target="tpu_custom_call" | custom-call | tf_op jit(solution)/shard_map/pack/pallas_call | solution.py:115
  1.9 54.1 %all_to_all.5.got_ref = bf16[256,9,2,128]{3,2,1,0:T(2,128)(2,1)S(1)} all-to-all(bf16[256,9,2,128]{3,2,1,0:T(2,128)(2,1)S(1)} %bitcast.8), channel_id=1, replica_groups={{0,1,2,3,4,5,6,7,8,9,10,11,12,13,14,15,16,17,18,19,20,21,22,23,24,25,26..., dimensions={0} | all-to-all | bytes 2359296 | tf_op jit(solution)/shard_map/all_to_all | solution.py:127
  56.0 0.5 regroup_theirs.1
  56.5 0.0 copy-start.2
  56.5 0.5 sum_theirs.1
  57.0 0.0 copy-start
  57.0 0.0 copy-start.1
  57.0 5.2 %collective-permute-start = (f32[512,128]{1,0:T(8,128)S(1)}, f32[512,128]{1,0:T(8,128)S(1)}, u32[]{:S(2)}, u32[]{:S(2)}) collective-permute-start(f32[512,128]{1,0:T(8,128)S(1)} %sum_theirs.1), channel_id=1, source_target_pairs={{0,32},{32,0},{64,96},{96,64},{128,160},{160,128},{192,224},{224,1... | collective-permute-start | bytes 786440 | tf_op jit(solution)/shard_map/ppermute | solution.py:162
  62.2 0.0 copy-done.2
  62.2 0.5 regroup_mine.1
  62.7 0.5 sum_mine.1.here
  63.2 0.1 collective-permute-done.there
  63.3 0.0 copy-done
  63.3 0.0 copy-done.1
  63.3 1.2 %update.1 = (f32[512,128]{1,0:T(8,128)}, f32[512,128]{1,0:T(8,128)}) custom-call(f32[512,128]{1,0:T(8,128)S(1)} %sum_mine.1.here, f32[512,128]{1,0:T(8,128)S(1)} %collective-permute-done.there, bf16[512,512]{1,0:T(8,128)(2,1)S(1)} %get-tuple-element.5.placing, f32[512,128]{1,0:T(8,128)S(1)} %copy-done, f32[512,128]{1,0:T(8,128)S(1)} %copy-done.1), custom_call_target="tpu_custom_call" | custom-call | tf_op jit(solution)/shard_map/update/pallas_call | solution.py:177
Async XLA Ops:
  56.5 5.7 %copy-start.2 = (s32[1,512]{1,0:T(1,128)S(1)}, s32[1,512]{1,0:T(1,128)}, u32[]{:S(2)}) copy-start(s32[1,512]{1,0:T(1,128)} %slots_ref.1) | copy-start | bytes 6148
  57.0 6.3 %copy-start = (f32[512,128]{1,0:T(8,128)S(1)}, f32[512,128]{1,0:T(8,128)}, u32[]{:S(2)}) copy-start(f32[512,128]{1,0:T(8,128)} %mom.1) | copy-start | bytes 786436
  57.0 6.3 %copy-start.1 = (f32[512,128]{1,0:T(8,128)S(1)}, f32[512,128]{1,0:T(8,128)}, u32[]{:S(2)}) copy-start(f32[512,128]{1,0:T(8,128)} %par.1) | copy-start | bytes 786436
  57.0 6.3 %collective-permute-start = (f32[512,128]{1,0:T(8,128)S(1)}, f32[512,128]{1,0:T(8,128)S(1)}, u32[]{:S(2)}, u32[]{:S(2)}) collective-permute-start(f32[512,128]{1,0:T(8,128)S(1)} %sum_theirs.1), channel_id=1, source_target_pairs={{0,32},{32,0},{64,96},{96,64},{128,160},{160,128},{192,224},{224,1... | collective-permute-start | bytes 786440 | tf_op jit(solution)/shard_map/ppermute | solution.py:162

commit v4 on v3

--- a/solution.py
+++ b/solution.py
@@ -131,7 +131,7 @@
         concat_axis=0,
         tiled=True,
         axis_index_groups=[
-            [(g * PAIR + side) * columns + b for g in range(pairs) for b in range(columns)]
+            [(g * PAIR + (g + b + side) % PAIR) * columns + b for g in range(pairs) for b in range(columns)]
             for side in range(PAIR)
         ],
     )

time: 64.8 us -> 64.4 us (level)
  starting transfers between devices: 5.16 us -> 2.66 us
  blocking collectives: 54.1 us -> 56.1 us
    ppermute x1, starting transfers between devices: 5.16 us -> 2.66 us  [shards(): lax.ppermute(summed(False, theirs, theirs), 'grp', [(g, g ^ 1) for g in r...]
    all_to_all x1, blocking collectives: 54.1 us -> 56.1 us  [shards(): lax.all_to_all(packed.reshape(sources, PAIR * tiles + 1, PAIR, block), ('...]
where the time goes in v4:
time: 64.4 us; the launch traced here: 64.1 us
  blocking collectives  56.1 us (87%)
  Pallas kernels  4.46 us (7%)
  starting transfers between devices  2.66 us (4%)
  between operations  0.71 us (1%)
    all_to_all x1, blocking collectives, shards(): lax.all_to_all(packed.reshape(sources, PAIR * tiles + 1, PAIR, block), ('...  56.1 us
    ppermute x1, starting transfers between devices, shards(): lax.ppermute(summed(False, theirs, theirs), 'grp', [(g, g ^ 1) for g in r...  2.66 us
  transfers between devices with their start and end apart: 1, of which 1 were waited for; matrix products, arithmetic and copies ran while one was open for 0% of the time, Pallas kernels for 2%

profile of v4, /device:TPU:1, one launch (start us, length us, event | category | flops | bytes accessed | tf_op | source)
XLA Modules:
  0.0 64.1 jit_solution(1224349989341233075)
XLA Ops:
  0.6 1.2 %pack.1 = bf16[8,32,9,2,128]{4,3,2,1,0:T(2,128)(2,1)S(1)} custom-call(bf16[8,2,32,4,2,128]{5,4,3,2,1,0:T(2,128)(2,1)} %bitcast.10, s32[32,128]{1,0:T(8,128)} %bitcast.11), custom_call_target="tpu_custom_call" | custom-call | tf_op jit(solution)/shard_map/pack/pallas_call | solution.py:115
  1.9 56.1 %all_to_all.5.got_ref = bf16[256,9,2,128]{3,2,1,0:T(2,128)(2,1)S(1)} all-to-all(bf16[256,9,2,128]{3,2,1,0:T(2,128)(2,1)S(1)} %bitcast.8), channel_id=1, replica_groups={{0,33,2,35,4,37,6,39,8,41,10,43,12,45,14,47,16,49,18,51,20,53,22,55,24,..., dimensions={0} | all-to-all | bytes 2359296 | tf_op jit(solution)/shard_map/all_to_all | solution.py:127
  58.0 0.5 regroup_theirs.1
  58.5 0.0 copy-start.2
  58.5 0.5 sum_theirs.1
  59.0 0.0 copy-start
  59.0 0.0 copy-start.1
  59.0 2.7 %collective-permute-start = (f32[512,128]{1,0:T(8,128)S(1)}, f32[512,128]{1,0:T(8,128)S(1)}, u32[]{:S(2)}, u32[]{:S(2)}) collective-permute-start(f32[512,128]{1,0:T(8,128)S(1)} %sum_theirs.1), channel_id=1, source_target_pairs={{0,32},{32,0},{64,96},{96,64},{128,160},{160,128},{192,224},{224,1... | collective-permute-start | bytes 786440 | tf_op jit(solution)/shard_map/ppermute | solution.py:162
  61.7 0.0 copy-done.2
  61.7 0.5 regroup_mine.1
  62.2 0.5 sum_mine.1.here
  62.7 0.1 collective-permute-done.there
  62.8 0.0 copy-done
  62.8 0.0 copy-done.1
  62.8 1.2 %update.1 = (f32[512,128]{1,0:T(8,128)}, f32[512,128]{1,0:T(8,128)}) custom-call(f32[512,128]{1,0:T(8,128)S(1)} %sum_mine.1.here, f32[512,128]{1,0:T(8,128)S(1)} %collective-permute-done.there, bf16[512,512]{1,0:T(8,128)(2,1)S(1)} %get-tuple-element.5.placing, f32[512,128]{1,0:T(8,128)S(1)} %copy-done, f32[512,128]{1,0:T(8,128)S(1)} %copy-done.1), custom_call_target="tpu_custom_call" | custom-call | tf_op jit(solution)/shard_map/update/pallas_call | solution.py:177
Async XLA Ops:
  58.5 3.2 %copy-start.2 = (s32[1,512]{1,0:T(1,128)S(1)}, s32[1,512]{1,0:T(1,128)}, u32[]{:S(2)}) copy-start(s32[1,512]{1,0:T(1,128)} %slots_ref.1) | copy-start | bytes 6148
  59.0 3.8 %copy-start = (f32[512,128]{1,0:T(8,128)S(1)}, f32[512,128]{1,0:T(8,128)}, u32[]{:S(2)}) copy-start(f32[512,128]{1,0:T(8,128)} %mom.1) | copy-start | bytes 786436
  59.0 3.8 %copy-start.1 = (f32[512,128]{1,0:T(8,128)S(1)}, f32[512,128]{1,0:T(8,128)}, u32[]{:S(2)}) copy-start(f32[512,128]{1,0:T(8,128)} %par.1) | copy-start | bytes 786436
  59.0 3.8 %collective-permute-start = (f32[512,128]{1,0:T(8,128)S(1)}, f32[512,128]{1,0:T(8,128)S(1)}, u32[]{:S(2)}, u32[]{:S(2)}) collective-permute-start(f32[512,128]{1,0:T(8,128)S(1)} %sum_theirs.1), channel_id=1, source_target_pairs={{0,32},{32,0},{64,96},{96,64},{128,160},{160,128},{192,224},{224,1... | collective-permute-start | bytes 786440 | tf_op jit(solution)/shard_map/ppermute | solution.py:162

commit v5 on v4

v5 whole, which is shorter than its diff:
```python
import functools

import jax
import jax.numpy as jnp
from jax import lax
from jax.experimental import pallas as pl
from jax.experimental.pallas import tpu as pltpu
from jax.sharding import PartitionSpec as P

PAIR = 2
VMEM_LIMIT = 16 * 1024 * 1024


def pack(tiles, window, grads_ref, picks_ref, out_ref, numbers_ref, sems):
    read = pltpu.make_async_copy(picks_ref, numbers_ref, sems.at[PAIR])
    copies = [
        pltpu.make_async_copy(
            grads_ref.at[:, side], out_ref.at[:, :, side * tiles : (side + 1) * tiles], sems.at[side]
        )
        for side in range(PAIR)
    ]
    read.start()
    for copy in copies:
        copy.start()
    read.wait()
    groups, columns = out_ref.shape[:2]
    rows = numbers_ref.shape[0] // (PAIR * groups)
    share = columns // rows
    offsets = lax.rem(numbers_ref[...], window).astype(jnp.float32)
    for g in range(groups):
        for r in range(rows):
            at = [(g * PAIR + side) * rows + r for side in range(PAIR)]
            two = jnp.concatenate([offsets[a : a + 1] for a in at], axis=0).astype(jnp.bfloat16)
            out_ref[g, r * share : (r + 1) * share, PAIR * tiles] = jnp.broadcast_to(
                two[None], (share,) + two.shape
            )
    for copy in copies:
        copy.wait()


def side_of():
    return lax.rem(lax.axis_index("grp"), PAIR)


def regroup(got_ref, slots_ref, out_ref, placing_ref, sems):
    copies = [
        pltpu.make_async_copy(got_ref.at[:, k], out_ref.at[k], sems.at[k]) for k in range(out_ref.shape[0])
    ]
    for copy in copies:
        copy.start()
    numbered = lax.broadcasted_iota(jnp.int32, placing_ref.shape, 0)
    placing_ref[...] = jnp.where(numbered == slots_ref[...], 1.0, 0.0).astype(jnp.bfloat16)
    for copy in copies:
        copy.wait()


def add_up(pick, window, share, got, here, there, numbers):
    tiles = pick // PAIR
    count = got.shape[1]
    numbers[...] = got[PAIR * tiles].astype(jnp.float32).T
    first = lax.rem(lax.axis_index("blk"), share) * pick
    both = numbers[pl.ds(pl.multiple_of(first, pick), pick), :]
    odd = lax.rem(lax.broadcasted_iota(jnp.int32, (1, count), 1), PAIR)
    place = lax.broadcasted_iota(jnp.int32, (PAIR * window, count), 0).astype(jnp.float32)
    core = side_of()
    beside = (pltpu.roll(both, 1, 1), pltpu.roll(both, count - 1, 1))
    for side, sums in ((1 - core, there), (core, here)):
        chosen = jnp.where(odd == side, both, jnp.where(side == 0, beside[0], beside[1]))
        for k in range(tiles):
            key = jnp.where(
                odd == 1, chosen[PAIR * k + 1 : PAIR * k + 2] + float(window), chosen[PAIR * k : PAIR * k + 1]
            )
            onehot = jnp.where(place == key, 1.0, 0.0).astype(jnp.bfloat16)
            sums[PAIR * window * k : PAIR * window * (k + 1)] = jnp.dot(
                onehot, got[side * tiles + k], preferred_element_type=jnp.float32
            )


def update(here, swapped, placing, mom, par, new_mom, new_par):
    owned, block = mom.shape
    other = pl.multiple_of((1 - side_of()) * owned, owned)
    merged = here[...] + swapped[pl.ds(other, owned), :]
    high = merged.astype(jnp.bfloat16)
    rest = merged - high.astype(jnp.float32)
    pieces = jnp.concatenate([high, rest.astype(jnp.bfloat16)], axis=1)
    sums = jnp.dot(placing[...], pieces, preferred_element_type=jnp.float32)
    gradient = sums[:, :block] + sums[:, block:]
    new_momentum = 0.9 * mom[...] + gradient
    new_mom[...] = new_momentum
    new_par[...] = par[...] - 0.05 * (gradient + 0.9 * new_momentum)


def shards(grads, picks, slot_map, momentum, params):
    groups, columns = lax.axis_size("grp"), lax.axis_size("blk")
    items, block = grads.shape[1:]
    owned = slot_map.shape[1]
    pick = items // (groups * columns)
    tiles = pick // PAIR
    window = owned // pick
    share = block // pick
    pairs = groups // PAIR
    sources = pairs * columns
    vmem = pl.BlockSpec(memory_space=pltpu.VMEM)
    distant = pl.BlockSpec(memory_space=pltpu.HBM)
    in_hbm = functools.partial(pltpu.with_memory_space_constraint, memory_space=pltpu.HBM)
    limits = pltpu.CompilerParams(vmem_limit_bytes=VMEM_LIMIT)
    packed = pl.pallas_call(
        functools.partial(pack, tiles, window),
        out_shape=jax.ShapeDtypeStruct((pairs, columns, PAIR * tiles + 1, PAIR, block), grads.dtype),
        in_specs=[distant, distant],
        out_specs=vmem,
        scratch_shapes=[pltpu.VMEM((items // block, block), jnp.int32), pltpu.SemaphoreType.DMA((PAIR + 1,))],
        compiler_params=limits,
        name="pack",
    )(
        in_hbm(grads.reshape(pairs, PAIR, columns, tiles, PAIR, block)),
        in_hbm(picks.reshape(items // block, block)),
    )
    arrived = lax.all_to_all(
        packed.reshape(sources, PAIR * tiles + 1, PAIR, block),
        ("grp", "blk"),
        split_axis=0,
        concat_axis=0,
        tiled=True,
        axis_index_groups=[
            [(g * PAIR + (g + b + side) % PAIR) * columns + b for g in range(pairs) for b in range(columns)]
            for side in range(PAIR)
        ],
    )

    grouped, placing = pl.pallas_call(
        regroup,
        out_shape=(
            jax.ShapeDtypeStruct((PAIR * tiles + 1, sources, PAIR, block), grads.dtype),
            jax.ShapeDtypeStruct((owned, owned), jnp.bfloat16),
        ),
        in_specs=[vmem, vmem],
        out_specs=(vmem, vmem),
        scratch_shapes=[pltpu.SemaphoreType.DMA((PAIR * tiles + 1,))],
        compiler_params=limits,
        name="regroup",
    )(arrived, slot_map)
    here, there = pl.pallas_call(
        functools.partial(add_up, pick, window, share),
        out_shape=(jax.ShapeDtypeStruct(momentum.shape, jnp.float32),) * 2,
        in_specs=[vmem],
        out_specs=(vmem, vmem),
        scratch_shapes=[pltpu.VMEM((block, PAIR * sources), jnp.float32)],
        compiler_params=limits,
        name="add_up",
    )(grouped.reshape(PAIR * tiles + 1, PAIR * sources, block))
    swapped = lax.all_gather(
        there,
        "grp",
        axis_index_groups=[[g, g + 1] for g in range(0, groups, PAIR)],
        tiled=True,
    )
    return pl.pallas_call(
        update,
        out_shape=(
            jax.ShapeDtypeStruct(momentum.shape, jnp.float32),
            jax.ShapeDtypeStruct(params.shape, jnp.float32),
        ),
        in_specs=[vmem] * 5,
        out_specs=(vmem, vmem),
        compiler_params=limits,
        name="update",
    )(here, swapped, placing, momentum, params)


def solution(mesh):
    placed = (
        P(("grp", "blk"), None, None),
        P(("grp", "blk"), None),
        P(("grp", "blk"), None),
        P(("grp", "blk"), None),
        P(("grp", "blk"), None),
    )
    return jax.shard_map(
        shards,
        mesh=mesh,
        in_specs=placed,
        out_specs=(P(("grp", "blk"), None), P(("grp", "blk"), None)),
        check_vma=False,
    )
```

time: 64.4 us -> 63.4 us (0.984)
  starting transfers between devices: 2.66 us -> 0 us
  blocking collectives: 56.1 us -> 58.5 us
    ppermute x1 -> x0, starting transfers between devices: 2.66 us -> none  [shards(): lax.ppermute(summed(False, theirs, theirs), 'grp', [(g, g ^ 1) for g in r...]
    all_gather x0 -> x1, blocking collectives: none -> 2.43 us  [shards(): lax.all_gather(there, 'grp', axis_index_groups=[[g, g + 1] for g in range...]
    pallas_call x4 -> x2, Pallas kernels: 1.97 us -> 1.6 us  [the longest x1 1.01 us: shards(): pl.pallas_call(regroup, out_shape=(jax.ShapeDtypeStruct((PAIR * tiles + 1...]
  transfers between devices with their start and end apart: 1 -> 0, of which waited for: 1 -> 0; matrix products, arithmetic and copies ran while one was open for 0% -> 0% of each run, Pallas kernels for 2% -> 0%
where the time goes in v5:
time: 63.4 us; the launch traced here: 63.2 us
  blocking collectives  58.5 us (92%)
  Pallas kernels  3.95 us (6%)
  between operations  0.68 us (1%)
    all_to_all x1, blocking collectives, shards(): lax.all_to_all(packed.reshape(sources, PAIR * tiles + 1, PAIR, block), ('...  56.1 us
    all_gather x1, blocking collectives, shards(): lax.all_gather(there, 'grp', axis_index_groups=[[g, g + 1] for g in range...  2.43 us

profile of v5, /device:TPU:1, one launch (start us, length us, event | category | flops | bytes accessed | tf_op | source)
XLA Modules:
  0.0 63.2 jit_solution(13258541014861477455)
XLA Ops:
  0.6 1.2 %pack.1 = bf16[8,32,9,2,128]{4,3,2,1,0:T(2,128)(2,1)S(1)} custom-call(bf16[8,2,32,4,2,128]{5,4,3,2,1,0:T(2,128)(2,1)} %bitcast.6, s32[32,128]{1,0:T(8,128)} %bitcast.7), custom_call_target="tpu_custom_call" | custom-call | tf_op jit(solution)/shard_map/pack/pallas_call | solution.py:107
  1.9 0.0 copy-start.2
  1.9 56.1 %all_to_all.5.got_ref = bf16[256,9,2,128]{3,2,1,0:T(2,128)(2,1)S(1)} all-to-all(bf16[256,9,2,128]{3,2,1,0:T(2,128)(2,1)S(1)} %bitcast.4), channel_id=1, replica_groups={{0,33,2,35,4,37,6,39,8,41,10,43,12,45,14,47,16,49,18,51,20,53,22,55,24,..., dimensions={0} | all-to-all | bytes 2359296 | tf_op jit(solution)/shard_map/all_to_all | solution.py:119
  58.0 0.0 copy-done.2
  58.0 1.0 %regroup.1 = (bf16[9,256,2,128]{3,2,1,0:T(2,128)(2,1)S(1)}, bf16[512,512]{1,0:T(8,128)(2,1)S(1)}) custom-call(bf16[256,9,2,128]{3,2,1,0:T(2,128)(2,1)S(1)} %all_to_all.5.got_ref, s32[1,512]{1,0:T(1,128)S(1)} %copy-done.2), custom_call_target="tpu_custom_call" | custom-call | tf_op jit(solution)/shard_map/regroup/pallas_call | solution.py:131
  59.0 0.0 copy-start
  59.0 0.0 copy-start.1
  59.0 0.6 add_up.1
  59.6 2.4 %all_gather.3.swapped = f32[1024,128]{1,0:T(8,128)S(1)} all-gather(f32[512,128]{1,0:T(8,128)S(1)} %get-tuple-element.8), channel_id=1, replica_groups={{0,32},{64,96},{128,160},{192,224},{256,288},{320,352},{384,416},{448,4..., dimensions={0}, use_global_device_ids=true | all-gather | bytes 786432 | tf_op jit(solution)/shard_map/all_gather | solution.py:152
  62.1 0.0 copy-done
  62.1 0.0 copy-done.1
  62.1 1.1 %update.1 = (f32[512,128]{1,0:T(8,128)}, f32[512,128]{1,0:T(8,128)}) custom-call(f32[512,128]{1,0:T(8,128)S(1)} %get-tuple-element.7.here, f32[1024,128]{1,0:T(8,128)S(1)} %all_gather.3.swapped, bf16[512,512]{1,0:T(8,128)(2,1)S(1)} %get-tuple-element.9.placing, f32[512,128]{1,0:T(8,128)S(1)} %copy-done, f32[512,128]{1,0:T(8,128)S(1)} %copy-done.1), custom_call_target="tpu_custom_call" | custom-call | tf_op jit(solution)/shard_map/update/pallas_call | solution.py:158
Async XLA Ops:
  1.9 56.1 %copy-start.2 = (s32[1,512]{1,0:T(1,128)S(1)}, s32[1,512]{1,0:T(1,128)}, u32[]{:S(2)}) copy-start(s32[1,512]{1,0:T(1,128)} %slots_ref.1) | copy-start | bytes 6148
  59.0 3.1 %copy-start = (f32[512,128]{1,0:T(8,128)S(1)}, f32[512,128]{1,0:T(8,128)}, u32[]{:S(2)}) copy-start(f32[512,128]{1,0:T(8,128)} %mom.1) | copy-start | bytes 786436
  59.0 3.0 %copy-start.1 = (f32[512,128]{1,0:T(8,128)S(1)}, f32[512,128]{1,0:T(8,128)}, u32[]{:S(2)}) copy-start(f32[512,128]{1,0:T(8,128)} %par.1) | copy-start | bytes 786436

commit v6 on v5

--- a/solution.py
+++ b/solution.py
@@ -42,24 +42,14 @@
     return lax.rem(lax.axis_index("grp"), PAIR)
 
 
-def regroup(got_ref, slots_ref, out_ref, placing_ref, sems):
-    copies = [
-        pltpu.make_async_copy(got_ref.at[:, k], out_ref.at[k], sems.at[k]) for k in range(out_ref.shape[0])
-    ]
-    for copy in copies:
-        copy.start()
-    numbered = lax.broadcasted_iota(jnp.int32, placing_ref.shape, 0)
-    placing_ref[...] = jnp.where(numbered == slots_ref[...], 1.0, 0.0).astype(jnp.bfloat16)
-    for copy in copies:
-        copy.wait()
-
-
-def add_up(pick, window, share, got, here, there, numbers):
+def add_up(pick, window, share, got, slots, here, there, placing, numbers):
     tiles = pick // PAIR
     count = got.shape[1]
     numbers[...] = got[PAIR * tiles].astype(jnp.float32).T
     first = lax.rem(lax.axis_index("blk"), share) * pick
     both = numbers[pl.ds(pl.multiple_of(first, pick), pick), :]
+    numbered = lax.broadcasted_iota(jnp.int32, placing.shape, 0)
+    placing[...] = jnp.where(numbered == slots[...], 1.0, 0.0).astype(jnp.bfloat16)
     odd = lax.rem(lax.broadcasted_iota(jnp.int32, (1, count), 1), PAIR)
     place = lax.broadcasted_iota(jnp.int32, (PAIR * window, count), 0).astype(jnp.float32)
     core = side_of()
@@ -128,27 +118,20 @@
         ],
     )
 
-    grouped, placing = pl.pallas_call(
-        regroup,
+    grouped = jnp.swapaxes(arrived, 0, 1).reshape(PAIR * tiles + 1, PAIR * sources, block)
+    here, there, placing = pl.pallas_call(
+        functools.partial(add_up, pick, window, share),
         out_shape=(
-            jax.ShapeDtypeStruct((PAIR * tiles + 1, sources, PAIR, block), grads.dtype),
+            jax.ShapeDtypeStruct(momentum.shape, jnp.float32),
+            jax.ShapeDtypeStruct(momentum.shape, jnp.float32),
             jax.ShapeDtypeStruct((owned, owned), jnp.bfloat16),
         ),
         in_specs=[vmem, vmem],
-        out_specs=(vmem, vmem),
-        scratch_shapes=[pltpu.SemaphoreType.DMA((PAIR * tiles + 1,))],
-        compiler_params=limits,
-        name="regroup",
-    )(arrived, slot_map)
-    here, there = pl.pallas_call(
-        functools.partial(add_up, pick, window, share),
-        out_shape=(jax.ShapeDtypeStruct(momentum.shape, jnp.float32),) * 2,
-        in_specs=[vmem],
-        out_specs=(vmem, vmem),
+        out_specs=(vmem, vmem, vmem),
         scratch_shapes=[pltpu.VMEM((block, PAIR * sources), jnp.float32)],
         compiler_params=limits,
         name="add_up",
-    )(grouped.reshape(PAIR * tiles + 1, PAIR * sources, block))
+    )(grouped, slot_map)
     swapped = lax.all_gather(
         there,
         "grp",

time: 63.4 us -> 63.4 us (level)
  Pallas kernels: 3.95 us -> 3.03 us
  local copies, waits for them, and re-layouts: 0.02 us -> 0.92 us
    pallas_call x1 -> x0, Pallas kernels: 1.01 us -> none  [shards(): pl.pallas_call(regroup, out_shape=(jax.ShapeDtypeStruct((PAIR * tiles + 1...]
    transpose x0 -> x1, local copies, waits for them, and re-layouts: none -> 0.91 us  [shards(): jnp.swapaxes(arrived, 0, 1).reshape(PAIR * tiles + 1, PAIR * sources, block)]
where the time goes in v6:
time: 63.4 us; the launch traced here: 63.1 us
  blocking collectives  58.5 us (92%)
  Pallas kernels  3.03 us (5%)
  local copies, waits for them, and re-layouts  0.92 us (1%)
  between operations  0.68 us (1%)
    all_to_all x1, blocking collectives, shards(): lax.all_to_all(packed.reshape(sources, PAIR * tiles + 1, PAIR, block), ('...  56.1 us
    all_gather x1, blocking collectives, shards(): lax.all_gather(there, 'grp', axis_index_groups=[[g, g + 1] for g in range...  2.44 us

profile of v6, /device:TPU:1, one launch (start us, length us, event | category | flops | bytes accessed | tf_op | source)
XLA Modules:
  0.0 63.1 jit_solution(3132202714907264678)
XLA Ops:
  0.6 1.2 %pack.1 = bf16[8,32,9,2,128]{4,3,2,1,0:T(2,128)(2,1)S(1)} custom-call(bf16[8,2,32,4,2,128]{5,4,3,2,1,0:T(2,128)(2,1)} %bitcast.8, s32[32,128]{1,0:T(8,128)} %bitcast.9), custom_call_target="tpu_custom_call" | custom-call | tf_op jit(solution)/shard_map/pack/pallas_call | solution.py:97
  1.9 56.1 %all_to_all.5 = bf16[256,9,2,128]{3,2,1,0:T(2,128)(2,1)S(1)} all-to-all(bf16[256,9,2,128]{3,2,1,0:T(2,128)(2,1)S(1)} %bitcast.6), channel_id=1, replica_groups={{0,33,2,35,4,37,6,39,8,41,10,43,12,45,14,47,16,49,18,51,20,53,22,55,24,..., dimensions={0} | all-to-all | bytes 2359296 | tf_op jit(solution)/shard_map/all_to_all | solution.py:109
  58.0 0.0 copy-start.2
  58.0 0.9 %copy.8 = bf16[9,256,2,128]{3,2,1,0:T(2,128)(2,1)S(1)} copy(bf16[9,256,2,128]{3,2,0,1:T(2,128)(2,1)S(1)} %bitcast.7) | data formatting | bytes 2359296 | tf_op jit(solution)/shard_map/transpose | solution.py:121
  58.9 0.0 copy-start
  58.9 0.0 copy-start.1
  58.9 0.0 copy-done.2
  58.9 0.7 %add_up.1 = (f32[512,128]{1,0:T(8,128)S(1)}, f32[512,128]{1,0:T(8,128)S(1)}, bf16[512,512]{1,0:T(8,128)(2,1)S(1)}) custom-call(bf16[9,512,128]{2,1,0:T(8,128)(2,1)S(1)} %bitcast.5, s32[1,512]{1,0:T(1,128)S(1)} %copy-done.2), custom_call_target="tpu_custom_call" | custom-call | tf_op jit(solution)/shard_map/add_up/pallas_call | solution.py:122
  59.6 2.4 %all_gather.3.swapped = f32[1024,128]{1,0:T(8,128)S(1)} all-gather(f32[512,128]{1,0:T(8,128)S(1)} %get-tuple-element.6), channel_id=1, replica_groups={{0,32},{64,96},{128,160},{192,224},{256,288},{320,352},{384,416},{448,4..., dimensions={0}, use_global_device_ids=true | all-gather | bytes 786432 | tf_op jit(solution)/shard_map/all_gather | solution.py:135
  62.0 0.0 copy-done
  62.0 0.0 copy-done.1
  62.0 1.1 %update.1 = (f32[512,128]{1,0:T(8,128)}, f32[512,128]{1,0:T(8,128)}) custom-call(f32[512,128]{1,0:T(8,128)S(1)} %get-tuple-element.5.here, f32[1024,128]{1,0:T(8,128)S(1)} %all_gather.3.swapped, bf16[512,512]{1,0:T(8,128)(2,1)S(1)} %get-tuple-element.7.placing, f32[512,128]{1,0:T(8,128)S(1)} %copy-done, f32[512,128]{1,0:T(8,128)S(1)} %copy-done.1), custom_call_target="tpu_custom_call" | custom-call | tf_op jit(solution)/shard_map/update/pallas_call | solution.py:141
Async XLA Ops:
  58.0 0.9 %copy-start.2 = (s32[1,512]{1,0:T(1,128)S(1)}, s32[1,512]{1,0:T(1,128)}, u32[]{:S(2)}) copy-start(s32[1,512]{1,0:T(1,128)} %slots.1) | copy-start | bytes 6148
  58.9 3.2 %copy-start = (f32[512,128]{1,0:T(8,128)S(1)}, f32[512,128]{1,0:T(8,128)}, u32[]{:S(2)}) copy-start(f32[512,128]{1,0:T(8,128)} %mom.1) | copy-start | bytes 786436
  58.9 3.1 %copy-start.1 = (f32[512,128]{1,0:T(8,128)S(1)}, f32[512,128]{1,0:T(8,128)}, u32[]{:S(2)}) copy-start(f32[512,128]{1,0:T(8,128)} %par.1) | copy-start | bytes 786436

commit v7 on v6

--- a/solution.py
+++ b/solution.py
@@ -42,14 +42,17 @@
     return lax.rem(lax.axis_index("grp"), PAIR)
 
 
-def add_up(pick, window, share, got, slots, here, there, placing, numbers):
+def place(slots, placing):
+    numbered = lax.broadcasted_iota(jnp.int32, placing.shape, 0)
+    placing[...] = jnp.where(numbered == slots[...], 1.0, 0.0).astype(jnp.bfloat16)
+
+
+def add_up(pick, window, share, got, here, there, numbers):
     tiles = pick // PAIR
     count = got.shape[1]
     numbers[...] = got[PAIR * tiles].astype(jnp.float32).T
     first = lax.rem(lax.axis_index("blk"), share) * pick
     both = numbers[pl.ds(pl.multiple_of(first, pick), pick), :]
-    numbered = lax.broadcasted_iota(jnp.int32, placing.shape, 0)
-    placing[...] = jnp.where(numbered == slots[...], 1.0, 0.0).astype(jnp.bfloat16)
     odd = lax.rem(lax.broadcasted_iota(jnp.int32, (1, count), 1), PAIR)
     place = lax.broadcasted_iota(jnp.int32, (PAIR * window, count), 0).astype(jnp.float32)
     core = side_of()
@@ -117,21 +120,28 @@
             for side in range(PAIR)
         ],
     )
+    placing = pl.pallas_call(
+        place,
+        out_shape=jax.ShapeDtypeStruct((owned, owned), jnp.bfloat16),
+        in_specs=[vmem],
+        out_specs=vmem,
+        compiler_params=limits,
+        name="place",
+    )(slot_map)
 
     grouped = jnp.swapaxes(arrived, 0, 1).reshape(PAIR * tiles + 1, PAIR * sources, block)
-    here, there, placing = pl.pallas_call(
+    here, there = pl.pallas_call(
         functools.partial(add_up, pick, window, share),
         out_shape=(
             jax.ShapeDtypeStruct(momentum.shape, jnp.float32),
             jax.ShapeDtypeStruct(momentum.shape, jnp.float32),
-            jax.ShapeDtypeStruct((owned, owned), jnp.bfloat16),
         ),
-        in_specs=[vmem, vmem],
-        out_specs=(vmem, vmem, vmem),
+        in_specs=[vmem],
+        out_specs=(vmem, vmem),
         scratch_shapes=[pltpu.VMEM((block, PAIR * sources), jnp.float32)],
         compiler_params=limits,
         name="add_up",
-    )(grouped, slot_map)
+    )(grouped)
     swapped = lax.all_gather(
         there,
         "grp",

time: 63.4 us -> 64.6 us (1.019)
  blocking collectives: 58.5 us -> 2.43 us
  waiting for transfers between devices: 0 us -> 32.7 us
  starting transfers between devices: 0 us -> 23.5 us
  Pallas kernels: 3.03 us -> 4.05 us
    all_to_all x1 -> x0, blocking collectives: 56.1 us -> none  [shards(): lax.all_to_all(packed.reshape(sources, PAIR * tiles + 1, PAIR, block), ('...]
    all_to_all x0 -> x1, waiting for transfers between devices: none -> 32.7 us  [shards(): lax.all_to_all(packed.reshape(sources, PAIR * tiles + 1, PAIR, block), ('...]
    all_to_all x0 -> x1, starting transfers between devices: none -> 23.5 us  [shards(): lax.all_to_all(packed.reshape(sources, PAIR * tiles + 1, PAIR, block), ('...]
    pallas_call x1, Pallas kernels: 1.24 us -> 2.26 us  [shards(): pl.pallas_call(functools.partial(pack, tiles, window), out_shape=jax.Shap...]
  transfers between devices with their start and end apart: 0 -> 1, of which waited for: 0 -> 1; matrix products, arithmetic and copies ran while one was open for 0% -> 0% of each run, Pallas kernels for 0% -> 0%
where the time goes in v7:
time: 64.6 us; the launch traced here: 64.3 us
  waiting for transfers between devices  32.7 us (51%)
  starting transfers between devices  23.5 us (36%)
  Pallas kernels  4.05 us (6%)
  blocking collectives  2.43 us (4%)
  local copies, waits for them, and re-layouts  0.92 us (1%)
  between operations  0.7 us (1%)
    all_to_all x1, waiting for transfers between devices, shards(): lax.all_to_all(packed.reshape(sources, PAIR * tiles + 1, PAIR, block), ('...  32.7 us
    all_to_all x1, starting transfers between devices, shards(): lax.all_to_all(packed.reshape(sources, PAIR * tiles + 1, PAIR, block), ('...  23.5 us
    all_gather x1, blocking collectives, shards(): lax.all_gather(there, 'grp', axis_index_groups=[[g, g + 1] for g in range...  2.43 us
    pallas_call x1, Pallas kernels, shards(): pl.pallas_call(functools.partial(pack, tiles, window), out_shape=jax.Shap...  2.26 us
  transfers between devices with their start and end apart: 1, of which 1 were waited for; matrix products, arithmetic and copies ran while one was open for 0% of the time, Pallas kernels for 0%

profile of v7, /device:TPU:1, one launch (start us, length us, event | category | flops | bytes accessed | tf_op | source)
XLA Modules:
  0.0 64.3 jit_solution(3429039428869293173)
XLA Ops:
  0.6 2.3 %pack.1 = bf16[8,32,9,2,128]{4,3,2,1,0:T(2,128)(2,1)} custom-call(bf16[8,2,32,4,2,128]{5,4,3,2,1,0:T(2,128)(2,1)} %bitcast.7, s32[32,128]{1,0:T(8,128)} %bitcast.8), custom_call_target="tpu_custom_call" | custom-call | tf_op jit(solution)/shard_map/pack/pallas_call | solution.py:100
  2.9 0.0 copy-start.2
  2.9 23.5 %all-to-all-start = ((bf16[256,9,2,128]{3,2,1,0:T(2,128)(2,1)}), bf16[256,9,2,128]{3,2,1,0:T(2,128)(2,1)S(1)}, u32[]{:S(2)}, u32[]{:S(2)}) async-start(bf16[256,9,2,128]{3,2,1,0:T(2,128)(2,1)} %bitcast.2), calls=%async_computation | async-start | bytes 2359296 | tf_op jit(solution)/shard_map/all_to_all | solution.py:112
  26.4 0.0 copy-done.2
  26.4 0.1 place.1.placing
  26.5 32.7 %all-to-all-done = bf16[256,9,2,128]{3,2,1,0:T(2,128)(2,1)S(1)} async-done(((bf16[256,9,2,128]{3,2,1,0:T(2,128)(2,1)}), bf16[256,9,2,128]{3,2,1,0:T(2,128)(2,1)S(1)}, u32[]{:S(2)}, u32[]{:S(2)}) %all-to-all-start) | async-done | bytes 1179680 | tf_op jit(solution)/shard_map/all_to_all | solution.py:112
  59.2 0.9 %copy.8 = bf16[9,256,2,128]{3,2,1,0:T(2,128)(2,1)S(1)} copy(bf16[9,256,2,128]{3,2,0,1:T(2,128)(2,1)S(1)} %bitcast.6) | data formatting | bytes 2359296 | tf_op jit(solution)/shard_map/transpose | solution.py:132
  60.1 0.0 copy-start
  60.1 0.0 copy-start.1
  60.2 0.6 add_up.1
  60.7 2.4 %all_gather.3.swapped = f32[1024,128]{1,0:T(8,128)S(1)} all-gather(f32[512,128]{1,0:T(8,128)S(1)} %get-tuple-element.5), channel_id=1, replica_groups={{0,32},{64,96},{128,160},{192,224},{256,288},{320,352},{384,416},{448,4..., dimensions={0}, use_global_device_ids=true | all-gather | bytes 786432 | tf_op jit(solution)/shard_map/all_gather | solution.py:145
  63.2 0.0 copy-done
  63.2 0.0 copy-done.1
  63.2 1.1 %update.1 = (f32[512,128]{1,0:T(8,128)}, f32[512,128]{1,0:T(8,128)}) custom-call(f32[512,128]{1,0:T(8,128)S(1)} %get-tuple-element.4.here, f32[1024,128]{1,0:T(8,128)S(1)} %all_gather.3.swapped, bf16[512,512]{1,0:T(8,128)(2,1)S(1)} %place.1.placing, f32[512,128]{1,0:T(8,128)S(1)} %copy-done, f32[512,128]{1,0:T(8,128)S(1)} %copy-done.1), custom_call_target="tpu_custom_call" | custom-call | tf_op jit(solution)/shard_map/update/pallas_call | solution.py:151
Async XLA Ops:
  2.9 23.5 %copy-start.2 = (s32[1,512]{1,0:T(1,128)S(1)}, s32[1,512]{1,0:T(1,128)}, u32[]{:S(2)}) copy-start(s32[1,512]{1,0:T(1,128)} %slots.1) | copy-start | bytes 6148
  2.9 56.3 %all-to-all-start = ((bf16[256,9,2,128]{3,2,1,0:T(2,128)(2,1)}), bf16[256,9,2,128]{3,2,1,0:T(2,128)(2,1)S(1)}, u32[]{:S(2)}, u32[]{:S(2)}) async-start(bf16[256,9,2,128]{3,2,1,0:T(2,128)(2,1)} %bitcast.2), calls=%async_computation | async-start | bytes 2359296 | tf_op jit(solution)/shard_map/all_to_all | solution.py:112
  60.1 3.1 %copy-start = (f32[512,128]{1,0:T(8,128)S(1)}, f32[512,128]{1,0:T(8,128)}, u32[]{:S(2)}) copy-start(f32[512,128]{1,0:T(8,128)} %mom.1) | copy-start | bytes 786436
  60.1 3.0 %copy-start.1 = (f32[512,128]{1,0:T(8,128)S(1)}, f32[512,128]{1,0:T(8,128)}, u32[]{:S(2)}) copy-start(f32[512,128]{1,0:T(8,128)} %par.1) | copy-start | bytes 786436

commit v8 on v6

--- a/solution.py
+++ b/solution.py
@@ -8,6 +8,7 @@
 from jax.sharding import PartitionSpec as P
 
 PAIR = 2
+ALONG_X = 4
 VMEM_LIMIT = 16 * 1024 * 1024
 
 
@@ -113,7 +114,11 @@
         concat_axis=0,
         tiled=True,
         axis_index_groups=[
-            [(g * PAIR + (g + b + side) % PAIR) * columns + b for g in range(pairs) for b in range(columns)]
+            [
+                (g * PAIR + (g + b // ALONG_X + b % ALONG_X + side) % PAIR) * columns + b
+                for g in range(pairs)
+                for b in range(columns)
+            ]
             for side in range(PAIR)
         ],
     )

time: 63.4 us -> 64.5 us (1.017)
  blocking collectives: 58.5 us -> 59.7 us
    all_to_all x1, blocking collectives: 56.1 us -> 57.5 us  [shards(): lax.all_to_all(packed.reshape(sources, PAIR * tiles + 1, PAIR, block), ('...]
where the time goes in v8:
time: 64.5 us; the launch traced here: 64.3 us
  blocking collectives  59.7 us (93%)
  Pallas kernels  3.03 us (5%)
  local copies, waits for them, and re-layouts  0.92 us (1%)
  between operations  0.68 us (1%)
    all_to_all x1, blocking collectives, shards(): lax.all_to_all(packed.reshape(sources, PAIR * tiles + 1, PAIR, block), ('...  57.5 us
    all_gather x1, blocking collectives, shards(): lax.all_gather(there, 'grp', axis_index_groups=[[g, g + 1] for g in range...  2.18 us

profile of v8, /device:TPU:1, one launch (start us, length us, event | category | flops | bytes accessed | tf_op | source)
XLA Modules:
  0.0 64.3 jit_solution(10537608412957231068)
XLA Ops:
  0.6 1.2 %pack.1 = bf16[8,32,9,2,128]{4,3,2,1,0:T(2,128)(2,1)S(1)} custom-call(bf16[8,2,32,4,2,128]{5,4,3,2,1,0:T(2,128)(2,1)} %bitcast.8, s32[32,128]{1,0:T(8,128)} %bitcast.9), custom_call_target="tpu_custom_call" | custom-call | tf_op jit(solution)/shard_map/pack/pallas_call | solution.py:98
  1.9 57.5 %all_to_all.5 = bf16[256,9,2,128]{3,2,1,0:T(2,128)(2,1)S(1)} all-to-all(bf16[256,9,2,128]{3,2,1,0:T(2,128)(2,1)S(1)} %bitcast.6), channel_id=1, replica_groups={{0,33,2,35,36,5,38,7,8,41,10,43,44,13,46,15,16,49,18,51,52,21,54,23,24,..., dimensions={0} | all-to-all | bytes 2359296 | tf_op jit(solution)/shard_map/all_to_all | solution.py:110
  59.4 0.0 copy-start.2
  59.4 0.9 %copy.8 = bf16[9,256,2,128]{3,2,1,0:T(2,128)(2,1)S(1)} copy(bf16[9,256,2,128]{3,2,0,1:T(2,128)(2,1)S(1)} %bitcast.7) | data formatting | bytes 2359296 | tf_op jit(solution)/shard_map/transpose | solution.py:126
  60.3 0.0 copy-start
  60.3 0.0 copy-start.1
  60.3 0.0 copy-done.2
  60.3 0.7 %add_up.1 = (f32[512,128]{1,0:T(8,128)S(1)}, f32[512,128]{1,0:T(8,128)S(1)}, bf16[512,512]{1,0:T(8,128)(2,1)S(1)}) custom-call(bf16[9,512,128]{2,1,0:T(8,128)(2,1)S(1)} %bitcast.5, s32[1,512]{1,0:T(1,128)S(1)} %copy-done.2), custom_call_target="tpu_custom_call" | custom-call | tf_op jit(solution)/shard_map/add_up/pallas_call | solution.py:127
  61.0 2.2 %all_gather.3.swapped = f32[1024,128]{1,0:T(8,128)S(1)} all-gather(f32[512,128]{1,0:T(8,128)S(1)} %get-tuple-element.6), channel_id=1, replica_groups={{0,32},{64,96},{128,160},{192,224},{256,288},{320,352},{384,416},{448,4..., dimensions={0}, use_global_device_ids=true | all-gather | bytes 786432 | tf_op jit(solution)/shard_map/all_gather | solution.py:140
  63.2 0.0 copy-done
  63.2 0.0 copy-done.1
  63.2 1.1 %update.1 = (f32[512,128]{1,0:T(8,128)}, f32[512,128]{1,0:T(8,128)}) custom-call(f32[512,128]{1,0:T(8,128)S(1)} %get-tuple-element.5.here, f32[1024,128]{1,0:T(8,128)S(1)} %all_gather.3.swapped, bf16[512,512]{1,0:T(8,128)(2,1)S(1)} %get-tuple-element.7.placing, f32[512,128]{1,0:T(8,128)S(1)} %copy-done, f32[512,128]{1,0:T(8,128)S(1)} %copy-done.1), custom_call_target="tpu_custom_call" | custom-call | tf_op jit(solution)/shard_map/update/pallas_call | solution.py:146
Async XLA Ops:
  59.4 0.9 %copy-start.2 = (s32[1,512]{1,0:T(1,128)S(1)}, s32[1,512]{1,0:T(1,128)}, u32[]{:S(2)}) copy-start(s32[1,512]{1,0:T(1,128)} %slots.1) | copy-start | bytes 6148
  60.3 2.9 %copy-start = (f32[512,128]{1,0:T(8,128)S(1)}, f32[512,128]{1,0:T(8,128)}, u32[]{:S(2)}) copy-start(f32[512,128]{1,0:T(8,128)} %mom.1) | copy-start | bytes 786436
  60.3 2.9 %copy-start.1 = (f32[512,128]{1,0:T(8,128)S(1)}, f32[512,128]{1,0:T(8,128)}, u32[]{:S(2)}) copy-start(f32[512,128]{1,0:T(8,128)} %par.1) | copy-start | bytes 786436

commit v9 on v8

--- a/solution.py
+++ b/solution.py
@@ -8,31 +8,36 @@
 from jax.sharding import PartitionSpec as P
 
 PAIR = 2
-ALONG_X = 4
 VMEM_LIMIT = 16 * 1024 * 1024
 
 
 def pack(tiles, window, grads_ref, picks_ref, out_ref, numbers_ref, sems):
-    read = pltpu.make_async_copy(picks_ref, numbers_ref, sems.at[PAIR])
+    groups, columns = out_ref.shape[:2]
+    at = lax.axis_index("grp")
+    group = lax.rem(lax.rem(at, PAIR) + at // PAIR + lax.axis_index("blk"), PAIR)
+    spots = [jnp.where(group == 0, g, groups - 1 - g) for g in range(groups)]
+    read = pltpu.make_async_copy(picks_ref, numbers_ref, sems.at[PAIR * groups])
     copies = [
         pltpu.make_async_copy(
-            grads_ref.at[:, side], out_ref.at[:, :, side * tiles : (side + 1) * tiles], sems.at[side]
+            grads_ref.at[g, side],
+            out_ref.at[spots[g], :, side * tiles : (side + 1) * tiles],
+            sems.at[g * PAIR + side],
         )
+        for g in range(groups)
         for side in range(PAIR)
     ]
     read.start()
     for copy in copies:
         copy.start()
     read.wait()
-    groups, columns = out_ref.shape[:2]
     rows = numbers_ref.shape[0] // (PAIR * groups)
     share = columns // rows
     offsets = lax.rem(numbers_ref[...], window).astype(jnp.float32)
     for g in range(groups):
         for r in range(rows):
-            at = [(g * PAIR + side) * rows + r for side in range(PAIR)]
-            two = jnp.concatenate([offsets[a : a + 1] for a in at], axis=0).astype(jnp.bfloat16)
-            out_ref[g, r * share : (r + 1) * share, PAIR * tiles] = jnp.broadcast_to(
+            lines = [(g * PAIR + side) * rows + r for side in range(PAIR)]
+            two = jnp.concatenate([offsets[a : a + 1] for a in lines], axis=0).astype(jnp.bfloat16)
+            out_ref[spots[g], r * share : (r + 1) * share, PAIR * tiles] = jnp.broadcast_to(
                 two[None], (share,) + two.shape
             )
     for copy in copies:
@@ -100,7 +105,7 @@
         out_shape=jax.ShapeDtypeStruct((pairs, columns, PAIR * tiles + 1, PAIR, block), grads.dtype),
         in_specs=[distant, distant],
         out_specs=vmem,
-        scratch_shapes=[pltpu.VMEM((items // block, block), jnp.int32), pltpu.SemaphoreType.DMA((PAIR + 1,))],
+        scratch_shapes=[pltpu.VMEM((items // block, block), jnp.int32), pltpu.SemaphoreType.DMA((items // (columns * pick) + 1,))],
         compiler_params=limits,
         name="pack",
     )(
@@ -115,8 +120,8 @@
         tiled=True,
         axis_index_groups=[
             [
-                (g * PAIR + (g + b // ALONG_X + b % ALONG_X + side) % PAIR) * columns + b
-                for g in range(pairs)
+                (g * PAIR + (g + b + side) % PAIR) * columns + b
+                for g in (reversed(range(pairs)) if side else range(pairs))
                 for b in range(columns)
             ]
             for side in range(PAIR)

time: 64.5 us -> 62.7 us (0.972)
  blocking collectives: 59.7 us -> 57.7 us
    all_to_all x1, blocking collectives: 57.5 us -> 55.5 us  [shards(): lax.all_to_all(packed.reshape(sources, PAIR * tiles + 1, PAIR, block), ('...]
where the time goes in v9:
time: 62.7 us; the launch traced here: 62.5 us
  blocking collectives  57.7 us (92%)
  Pallas kernels  3.19 us (5%)
  local copies, waits for them, and re-layouts  0.92 us (1%)
  between operations  0.68 us (1%)
    all_to_all x1, blocking collectives, shards(): lax.all_to_all(packed.reshape(sources, PAIR * tiles + 1, PAIR, block), ('...  55.5 us
    all_gather x1, blocking collectives, shards(): lax.all_gather(there, 'grp', axis_index_groups=[[g, g + 1] for g in range...  2.18 us
    pallas_call x1, Pallas kernels, shards(): pl.pallas_call(functools.partial(pack, tiles, window), out_shape=jax.Shap...  1.41 us

profile of v9, /device:TPU:1, one launch (start us, length us, event | category | flops | bytes accessed | tf_op | source)
XLA Modules:
  0.0 62.5 jit_solution(3162842841353221070)
XLA Ops:
  0.6 1.4 %pack.1 = bf16[8,32,9,2,128]{4,3,2,1,0:T(2,128)(2,1)S(1)} custom-call(bf16[8,2,32,4,2,128]{5,4,3,2,1,0:T(2,128)(2,1)} %bitcast.8, s32[32,128]{1,0:T(8,128)} %bitcast.9), custom_call_target="tpu_custom_call" | custom-call | tf_op jit(solution)/shard_map/pack/pallas_call | solution.py:103
  2.0 55.5 %all_to_all.5 = bf16[256,9,2,128]{3,2,1,0:T(2,128)(2,1)S(1)} all-to-all(bf16[256,9,2,128]{3,2,1,0:T(2,128)(2,1)S(1)} %bitcast.6), channel_id=1, replica_groups={{0,33,2,35,4,37,6,39,8,41,10,43,12,45,14,47,16,49,18,51,20,53,22,55,24,..., dimensions={0} | all-to-all | bytes 2359296 | tf_op jit(solution)/shard_map/all_to_all | solution.py:115
  57.5 0.0 copy-start.2
  57.5 0.9 %copy.8 = bf16[9,256,2,128]{3,2,1,0:T(2,128)(2,1)S(1)} copy(bf16[9,256,2,128]{3,2,0,1:T(2,128)(2,1)S(1)} %bitcast.7) | data formatting | bytes 2359296 | tf_op jit(solution)/shard_map/transpose | solution.py:131
  58.4 0.0 copy-start
  58.5 0.0 copy-start.1
  58.5 0.0 copy-done.2
  58.5 0.7 %add_up.1 = (f32[512,128]{1,0:T(8,128)S(1)}, f32[512,128]{1,0:T(8,128)S(1)}, bf16[512,512]{1,0:T(8,128)(2,1)S(1)}) custom-call(bf16[9,512,128]{2,1,0:T(8,128)(2,1)S(1)} %bitcast.5, s32[1,512]{1,0:T(1,128)S(1)} %copy-done.2), custom_call_target="tpu_custom_call" | custom-call | tf_op jit(solution)/shard_map/add_up/pallas_call | solution.py:132
  59.2 2.2 %all_gather.3.swapped = f32[1024,128]{1,0:T(8,128)S(1)} all-gather(f32[512,128]{1,0:T(8,128)S(1)} %get-tuple-element.6), channel_id=1, replica_groups={{0,32},{64,96},{128,160},{192,224},{256,288},{320,352},{384,416},{448,4..., dimensions={0}, use_global_device_ids=true | all-gather | bytes 786432 | tf_op jit(solution)/shard_map/all_gather | solution.py:145
  61.3 0.0 copy-done
  61.3 0.0 copy-done.1
  61.3 1.1 %update.1 = (f32[512,128]{1,0:T(8,128)}, f32[512,128]{1,0:T(8,128)}) custom-call(f32[512,128]{1,0:T(8,128)S(1)} %get-tuple-element.5.here, f32[1024,128]{1,0:T(8,128)S(1)} %all_gather.3.swapped, bf16[512,512]{1,0:T(8,128)(2,1)S(1)} %get-tuple-element.7.placing, f32[512,128]{1,0:T(8,128)S(1)} %copy-done, f32[512,128]{1,0:T(8,128)S(1)} %copy-done.1), custom_call_target="tpu_custom_call" | custom-call | tf_op jit(solution)/shard_map/update/pallas_call | solution.py:151
Async XLA Ops:
  57.5 0.9 %copy-start.2 = (s32[1,512]{1,0:T(1,128)S(1)}, s32[1,512]{1,0:T(1,128)}, u32[]{:S(2)}) copy-start(s32[1,512]{1,0:T(1,128)} %slots.1) | copy-start | bytes 6148
  58.4 2.9 %copy-start = (f32[512,128]{1,0:T(8,128)S(1)}, f32[512,128]{1,0:T(8,128)}, u32[]{:S(2)}) copy-start(f32[512,128]{1,0:T(8,128)} %mom.1) | copy-start | bytes 786436
  58.5 2.9 %copy-start.1 = (f32[512,128]{1,0:T(8,128)S(1)}, f32[512,128]{1,0:T(8,128)}, u32[]{:S(2)}) copy-start(f32[512,128]{1,0:T(8,128)} %par.1) | copy-start | bytes 786436

commit v10 on v9

--- a/solution.py
+++ b/solution.py
@@ -11,11 +11,16 @@
 VMEM_LIMIT = 16 * 1024 * 1024
 
 
+def places(count):
+    listed = [i // 2 if i % 2 == 0 else count - 1 - i // 2 for i in range(count)]
+    return [listed.index(i) for i in range(count)]
+
+
 def pack(tiles, window, grads_ref, picks_ref, out_ref, numbers_ref, sems):
     groups, columns = out_ref.shape[:2]
     at = lax.axis_index("grp")
     group = lax.rem(lax.rem(at, PAIR) + at // PAIR + lax.axis_index("blk"), PAIR)
-    spots = [jnp.where(group == 0, g, groups - 1 - g) for g in range(groups)]
+    spots = [jnp.where(group == 0, p, groups - 1 - p) for p in places(groups)]
     read = pltpu.make_async_copy(picks_ref, numbers_ref, sems.at[PAIR * groups])
     copies = [
         pltpu.make_async_copy(
@@ -121,7 +126,7 @@
         axis_index_groups=[
             [
                 (g * PAIR + (g + b + side) % PAIR) * columns + b
-                for g in (reversed(range(pairs)) if side else range(pairs))
+                for g in sorted(range(pairs), key=places(pairs).__getitem__, reverse=bool(side))
                 for b in range(columns)
             ]
             for side in range(PAIR)

time: 62.7 us -> 62.6 us (level)
    all_to_all x1, blocking collectives: 55.5 us -> 53.3 us  [shards(): lax.all_to_all(packed.reshape(sources, PAIR * tiles + 1, PAIR, block), ('...]
    all_gather x1, blocking collectives: 2.18 us -> 4.29 us  [shards(): lax.all_gather(there, 'grp', axis_index_groups=[[g, g + 1] for g in range...]
where the time goes in v10:
time: 62.6 us; the launch traced here: 62.4 us
  blocking collectives  57.6 us (92%)
  Pallas kernels  3.19 us (5%)
  local copies, waits for them, and re-layouts  0.92 us (1%)
  between operations  0.68 us (1%)
    all_to_all x1, blocking collectives, shards(): lax.all_to_all(packed.reshape(sources, PAIR * tiles + 1, PAIR, block), ('...  53.3 us
    all_gather x1, blocking collectives, shards(): lax.all_gather(there, 'grp', axis_index_groups=[[g, g + 1] for g in range...  4.29 us
    pallas_call x1, Pallas kernels, shards(): pl.pallas_call(functools.partial(pack, tiles, window), out_shape=jax.Shap...  1.41 us

profile of v10, /device:TPU:1, one launch (start us, length us, event | category | flops | bytes accessed | tf_op | source)
XLA Modules:
  0.0 62.4 jit_solution(9338743375855661614)
XLA Ops:
  0.6 1.4 %pack.1 = bf16[8,32,9,2,128]{4,3,2,1,0:T(2,128)(2,1)S(1)} custom-call(bf16[8,2,32,4,2,128]{5,4,3,2,1,0:T(2,128)(2,1)} %bitcast.8, s32[32,128]{1,0:T(8,128)} %bitcast.9), custom_call_target="tpu_custom_call" | custom-call | tf_op jit(solution)/shard_map/pack/pallas_call | solution.py:108
  2.0 53.3 %all_to_all.5 = bf16[256,9,2,128]{3,2,1,0:T(2,128)(2,1)S(1)} all-to-all(bf16[256,9,2,128]{3,2,1,0:T(2,128)(2,1)S(1)} %bitcast.6), channel_id=1, replica_groups={{0,33,2,35,4,37,6,39,8,41,10,43,12,45,14,47,16,49,18,51,20,53,22,55,24,..., dimensions={0} | all-to-all | bytes 2359296 | tf_op jit(solution)/shard_map/all_to_all | solution.py:120
  55.4 0.0 copy-start.2
  55.4 0.9 %copy.8 = bf16[9,256,2,128]{3,2,1,0:T(2,128)(2,1)S(1)} copy(bf16[9,256,2,128]{3,2,0,1:T(2,128)(2,1)S(1)} %bitcast.7) | data formatting | bytes 2359296 | tf_op jit(solution)/shard_map/transpose | solution.py:136
  56.3 0.0 copy-start
  56.3 0.0 copy-start.1
  56.3 0.0 copy-done.2
  56.3 0.7 %add_up.1 = (f32[512,128]{1,0:T(8,128)S(1)}, f32[512,128]{1,0:T(8,128)S(1)}, bf16[512,512]{1,0:T(8,128)(2,1)S(1)}) custom-call(bf16[9,512,128]{2,1,0:T(8,128)(2,1)S(1)} %bitcast.5, s32[1,512]{1,0:T(1,128)S(1)} %copy-done.2), custom_call_target="tpu_custom_call" | custom-call | tf_op jit(solution)/shard_map/add_up/pallas_call | solution.py:137
  57.0 4.3 %all_gather.3.swapped = f32[1024,128]{1,0:T(8,128)S(1)} all-gather(f32[512,128]{1,0:T(8,128)S(1)} %get-tuple-element.6), channel_id=1, replica_groups={{0,32},{64,96},{128,160},{192,224},{256,288},{320,352},{384,416},{448,4..., dimensions={0}, use_global_device_ids=true | all-gather | bytes 786432 | tf_op jit(solution)/shard_map/all_gather | solution.py:150
  61.3 0.0 copy-done
  61.3 0.0 copy-done.1
  61.3 1.1 %update.1 = (f32[512,128]{1,0:T(8,128)}, f32[512,128]{1,0:T(8,128)}) custom-call(f32[512,128]{1,0:T(8,128)S(1)} %get-tuple-element.5.here, f32[1024,128]{1,0:T(8,128)S(1)} %all_gather.3.swapped, bf16[512,512]{1,0:T(8,128)(2,1)S(1)} %get-tuple-element.7.placing, f32[512,128]{1,0:T(8,128)S(1)} %copy-done, f32[512,128]{1,0:T(8,128)S(1)} %copy-done.1), custom_call_target="tpu_custom_call" | custom-call | tf_op jit(solution)/shard_map/update/pallas_call | solution.py:156
Async XLA Ops:
  55.4 0.9 %copy-start.2 = (s32[1,512]{1,0:T(1,128)S(1)}, s32[1,512]{1,0:T(1,128)}, u32[]{:S(2)}) copy-start(s32[1,512]{1,0:T(1,128)} %slots.1) | copy-start | bytes 6148
  56.3 5.0 %copy-start = (f32[512,128]{1,0:T(8,128)S(1)}, f32[512,128]{1,0:T(8,128)}, u32[]{:S(2)}) copy-start(f32[512,128]{1,0:T(8,128)} %mom.1) | copy-start | bytes 786436
  56.3 5.0 %copy-start.1 = (f32[512,128]{1,0:T(8,128)S(1)}, f32[512,128]{1,0:T(8,128)}, u32[]{:S(2)}) copy-start(f32[512,128]{1,0:T(8,128)} %par.1) | copy-start | bytes 786436
